TPU v7x, 128 devices: a whole 4x4x4 slice. The times are simulated.
128 devices in a mesh: replica: 16 (over z, y), model: 8 (over x, core).
Axes of the slice: x: 4, y: 4, z: 4, core: 2. Of those that a mesh axis runs over, the one named last changes fastest.
Arguments:
- slope_up: float32 [16, 1024, 4096], P('replica', None, 'model'), may hold values from -4 to 4
- slope_down: float32 [16, 4096, 1024], P('replica', 'model'), may hold values from -4 to 4
- slope_query: float32 [16, 1024, 1024], P('replica', None, 'model'), may hold values from -4 to 4
- slope_key: float32 [16, 1024, 1024], P('replica', None, 'model'), may hold values from -4 to 4
- slope_value: float32 [16, 1024, 1024], P('replica', None, 'model'), may hold values from -4 to 4
- slope_mixed: float32 [16, 1024, 1024], P('replica', 'model'), may hold values from -4 to 4
- slope_norm: float32 [16, 1024], P('replica'), may hold values from -8 to 8
- slope_bias: float32 [16, 1024], P('replica'), may hold values from -8 to 8
- param_up: float32 [1024, 4096], P('replica', 'model'), may hold values from -0.25 to 0.25
- param_down: float32 [4096, 1024], P('model', 'replica'), may hold values from -0.125 to 0.125
- param_query: float32 [1024, 1024], P('replica', 'model'), may hold values from -0.25 to 0.25
- param_key: float32 [1024, 1024], P('replica', 'model'), may hold values from -0.25 to 0.25
- param_value: float32 [1024, 1024], P('replica', 'model'), may hold values from -0.25 to 0.25
- param_mixed: float32 [1024, 1024], P('model', 'replica'), may hold values from -0.25 to 0.25
- param_norm: float32 [1024], P('replica'), may hold values from 0.25 to 1.75
- param_bias: float32 [1024], P('replica'), may hold values from -3 to 3
- state_up: float32 [1024, 4096], P('replica', 'model'), may hold values from 0.0001953125 to 0.001953125
- state_down: float32 [4096, 1024], P('model', 'replica'), may hold values from 4.8828126e-05 to 0.00048828125
- state_query: float32 [1024, 1024], P('replica', 'model'), may hold values from 0.0001953125 to 0.001953125
- state_key: float32 [1024, 1024], P('replica', 'model'), may hold values from 0.0001953125 to 0.001953125
- state_value: float32 [1024, 1024], P('replica', 'model'), may hold values from 0.0001953125 to 0.001953125
- state_mixed: float32 [1024, 1024], P('model', 'replica'), may hold values from 0.0001953125 to 0.001953125
- state_norm: float32 [1024], P('replica'), may hold values from 0.05 to 0.8
- state_bias: float32 [1024], P('replica'), may hold values from 0.05 to 0.8
Outputs:
- half_up: bfloat16 [1024, 4096], P(None, 'model')
- half_down: bfloat16 [4096, 1024], P('model')
- half_query: bfloat16 [1024, 1024], P(None, 'model')
- half_key: bfloat16 [1024, 1024], P(None, 'model')
- half_value: bfloat16 [1024, 1024], P(None, 'model')
- half_mixed: bfloat16 [1024, 1024], P('model')
- half_norm: bfloat16 [1024], replicated
- half_bias: bfloat16 [1024], replicated
- next_up: float32 [1024, 4096], P('replica', 'model')
- next_down: float32 [4096, 1024], P('model', 'replica')
- next_query: float32 [1024, 1024], P('replica', 'model')
- next_key: float32 [1024, 1024], P('replica', 'model')
- next_value: float32 [1024, 1024], P('replica', 'model')
- next_mixed: float32 [1024, 1024], P('model', 'replica')
- next_norm: float32 [1024], P('replica')
- next_bias: float32 [1024], P('replica')
- state_new_up: float32 [1024, 4096], P('replica', 'model')
- state_new_down: float32 [4096, 1024], P('model', 'replica')
- state_new_query: float32 [1024, 1024], P('replica', 'model')
- state_new_key: float32 [1024, 1024], P('replica', 'model')
- state_new_value: float32 [1024, 1024], P('replica', 'model')
- state_new_mixed: float32 [1024, 1024], P('model', 'replica')
- state_new_norm: float32 [1024], P('replica')
- state_new_bias: float32 [1024], P('replica')
All inputs are finite; a program needn't handle non-finite values.
Results may differ from a plain program's by a relative error of at most 0.001.
Values may be sent and summed in bfloat16 or wider, within the bound.
No kernel may reach another device: no remote copies, remote signals or barrier semaphores. Data moves between devices by JAX's collectives and lax.ppermute only.
A program may use at most 64 MiB of HBM per device.

v0:
```python
import jax
import jax.numpy as jnp
from jax import lax
from jax.experimental import pallas as pl
from jax.experimental.pallas import tpu as pltpu
from jax.sharding import PartitionSpec as P


learn_rate = 0.025
hold_rate = 0.7

B = 64
T = 12 * B + 8
COLS = ((0, 4), (4, 1), (5, 1), (6, 1), (7, 4), (11, 1))
CUT = 4 * 3 * B
AT_VALUE = CUT
AT_DOWN = AT_VALUE + 2 * B
AT_MIXED = AT_DOWN + 512
AT_LAST = AT_MIXED + 128
ROWS = AT_LAST + 8
SCALE = 8192.0
SCALE_VEC = 4096.0
ORDER = (0, 2, 1, 3)
NEAR = (0, 1, 3, 2)


def vmem(x):
    return pltpu.with_memory_space_constraint(x, pltpu.VMEM)


def hbm(x):
    return pltpu.with_memory_space_constraint(x, pltpu.HBM)


VM = pl.BlockSpec(memory_space=pltpu.VMEM)
SM = pl.BlockSpec(memory_space=pltpu.SMEM)
HB = pl.BlockSpec(memory_space=pltpu.HBM)
PARAMS = pltpu.CompilerParams(vmem_limit_bytes=24 << 20)


def send(x, stage, d):
    pairs = []
    for z in range(4):
        for y in range(4):
            for m in range(8):
                along_y = (m % 2 == 0) == (stage == 0)
                to = (z * 4 + (y + d) % 4) if along_y else ((z + d) % 4 * 4 + y)
                pairs.append(((z * 4 + y) * 8 + m, to * 8 + m))
    return lax.ppermute(x, ("replica", "model"), pairs)


def block_of(at_ref, f, s):
    c = at_ref[2]
    return f * (1 + 3 * c) + s * (4 - 3 * c)


def pack(place, slopes, distances):
    n = len(distances)

    def kernel(at_ref, up, query, key, value, down, mixed, norm, bias, out_a, out_b, down_s, mixed_s, norm_s, bias_s, sems):
        fi, c = at_ref[0], at_ref[2]
        used = [0]

        def copy(source, target):
            one = pltpu.make_async_copy(source, target, sems.at[used[0]])
            used[0] += 1
            one.start()
            return one

        first = [copy(down.at[0, pl.ds(k * 128, 128)], down_s.at[pl.ds(k * 128, 128)]) for k in range(4)]
        first += [copy(mixed.at[0], mixed_s), copy(norm, norm_s), copy(bias, bias_s)]
        rest = []
        for o, d in enumerate(distances):
            f = (fi + d) & 3
            for s in range(4):
                rows = pl.ds(pl.multiple_of(block_of(at_ref, f, s) * B, B), B)
                target = out_b.at[o, pl.ds(s // 2 * B, B), pl.ds(s % 2 * 128, 128)]
                rest.append(copy(value.at[rows], target))
            ends = [
                (up, slice(0, 256), slice(0, B), slice(0, 256)),
                (up, slice(256, 512), slice(B, 2 * B), slice(0, 256)),
                (query, slice(0, 128), slice(2 * B, 3 * B), slice(0, 128)),
                (key, slice(0, 128), slice(2 * B, 3 * B), slice(128, 256)),
            ]
            for ref, lanes, rows, to in ends:
                at = used[0]
                used[0] += 1

                def one(source, ref=ref, lanes=lanes, rows=rows, to=to, at=at, o=o):
                    return pltpu.make_async_copy(source, out_a.at[o, :, rows, to], sems.at[at])

                @pl.when(c == 0)
                def _(ref=ref, lanes=lanes, one=one, f=f):
                    one(ref.at[:, f, :, lanes]).start()

                @pl.when(c != 0)
                def _(ref=ref, lanes=lanes, one=one, f=f):
                    one(ref.at[f, :, :, lanes]).start()

                rest.append(one(ref.at[0, :, :, lanes]))
        lane = lax.broadcasted_iota(jnp.int32, (B, 128), 1)
        row = lax.broadcasted_iota(jnp.int32, (8, 128), 0)

        def spread(ref, rows, to_row, make):
            for o, d in enumerate(distances):
                f = (fi + d) & 3
                turn_l = jnp.where(c == 0, (f & 1) * 64, 0)
                turn_r = jnp.where(c == 0, 64 - (f & 1) * 64, 0)
                for h in range(2):
                    t_l = jnp.where(c == 0, h * 4 + (f >> 1), f * 2 + h)
                    t_r = jnp.where(c == 0, h * 4 + 2 + (f >> 1), f * 2 + h)
                    left = make(ref, pl.ds(pl.multiple_of(t_l * 128, 128), 128))
                    right = make(ref, pl.ds(pl.multiple_of(t_r * 128, 128), 128))
                    left, right = pltpu.roll(left, turn_l, 1), pltpu.roll(right, turn_r, 1)
                    out_b[o, to_row : to_row + rows, h * 128 : h * 128 + 128] = jnp.where(lane[:rows] < 64, left, right)

        for k in range(10):
            if k < 8 and k % 2 == 0:
                first[k // 2].wait()
            if k == 8:
                for one in first[4:]:
                    one.wait()
            ref, at = (down_s, k * B) if k < 8 else (mixed_s, (k - 8) * B)
            spread(ref, B, AT_DOWN - CUT + k * B, lambda ref, lanes: ref[at : at + B, lanes])

        def last(refs, at):
            n = jnp.broadcast_to(refs[0][0:1, at] * 0.5, (8, 128))
            b = jnp.broadcast_to(refs[1][0:1, at] * 0.5, (8, 128))
            return jnp.where(row == 0, n, jnp.where(row == 1, b, 0.0))

        spread((norm_s, bias_s), 8, AT_LAST - CUT, last)
        for one in rest:
            one.wait()

    f32 = jnp.float32
    up, query, key, value, *others = slopes
    blocks = [x.reshape(4, 4, B, -1) for x in (up, query, key)]
    return pl.pallas_call(
        kernel,
        in_specs=[SM] + [HB] * 8,
        out_specs=(VM, VM),
        out_shape=(pltpu.VMEM((n, 4, 3 * B, 256), f32), pltpu.VMEM((n, ROWS - CUT, 256), f32)),
        scratch_shapes=[
            pltpu.VMEM((512, 1024), f32),
            pltpu.VMEM((128, 1024), f32),
            pltpu.VMEM((1, 1024), f32),
            pltpu.VMEM((1, 1024), f32),
            pltpu.SemaphoreType.DMA((7 + 8 * n,)),
        ],
        compiler_params=PARAMS,
    )(place, *[hbm(x) for x in (*blocks, value[0], *others)])


def turn_kernel(at_ref, a, b, out):
    for s in range(4):
        e = pl.ds((s - at_ref[1]) & 3, 1)
        for k in range(6):
            at = s * 192 + k // 2 * B
            out[e, k * B : k * B + B, :] = a[at : at + B, k % 2 * 128 : k % 2 * 128 + 128][None]
        at = s // 2 * B
        out[e, 6 * B : 7 * B, :] = b[at : at + B, s % 2 * 128 : s % 2 * 128 + 128][None]
    at = AT_DOWN - CUT
    for h in range(2):
        lanes = slice(h * 128, h * 128 + 128)
        tiles = [b[at + k * 128 : at + k * 128 + 128, lanes].T for k in range(5)]
        last = b[AT_LAST - CUT :, lanes]
        for j in range(2):
            e = (2 * h + j - at_ref[1]) & 3
            for k, tile in enumerate(tiles):
                out[pl.ds(e, 1), (7 + k) * B : (8 + k) * B, :] = tile[None, j * B : j * B + B]
            out[pl.ds(e, 1), 12 * B :, :] = (last if j == 0 else pltpu.roll(last, 64, 1))[None]


def turn(place, a, b):
    return pl.pallas_call(
        turn_kernel,
        in_specs=[SM, VM, VM],
        out_specs=VM,
        out_shape=pltpu.VMEM((4, T, 128), jnp.float32),
        compiler_params=PARAMS,
        name="turn",
    )(place, vmem(a), vmem(b))


def norms_kernel(total, p_up, p_query, p_key, p_value, p_down, p_mixed, part):
    lane = lax.broadcasted_iota(jnp.int32, (B, 128), 1)
    params = (p_up, p_query, p_key, p_value, p_down, p_mixed)
    table = jnp.zeros((B, 128), jnp.float32)
    for m, (col, n) in enumerate(COLS):
        squares = jnp.zeros((B, 128), jnp.float32)
        own = jnp.zeros((B, 128), jnp.float32)
        for k in range(n):
            x = total[(col + k) * B : (col + k + 1) * B, :] * (1.0 / SCALE)
            squares = squares + x * x
            p = params[m][:, k * 128 : k * 128 + 128]
            own = own + p * p
        s = jnp.sum(squares, axis=1, keepdims=True)
        o = jnp.sum(own, axis=1, keepdims=True)
        table = jnp.where(lane == m, o, jnp.where(lane == 8 + m, s, table))
    table = jnp.concatenate([table, jnp.zeros((128 - B, 128), jnp.float32)], axis=0)
    table = table.T[:16, :]
    for r in range(part.shape[0]):
        part[r] = table


def norms(copies, total, *params):
    return pl.pallas_call(
        norms_kernel,
        in_specs=[VM] * 7,
        out_specs=VM,
        out_shape=pltpu.VMEM((copies, 16, 128), jnp.float32),
        compiler_params=PARAMS,
        name="norms",
    )(vmem(total), *params)


def steps(parts, total, params, states, store, store_half):
    sums = parts[0]
    for d in range(1, parts.shape[0]):
        sums = sums + parts[d]
    ratio = jnp.sqrt(sums[:8]) * lax.rsqrt(sums[8:16] + 1e-06)
    ratio = jnp.concatenate([ratio, jnp.zeros((120, 128), jnp.float32)], axis=0).T[:B, :]

    def step(m, param, state):
        new = hold_rate * state + (1.0 - hold_rate) * m * m
        return param - learn_rate * m * lax.rsqrt(new + 1e-06), new

    for i, (col, n) in enumerate(COLS):
        r = ratio[:, i : i + 1]
        for k in range(n):
            at = (col + k) * B
            lanes = slice(k * 128, k * 128 + 128)
            m = total[at : at + B, :] * (1.0 / SCALE) * r
            nxt, new = step(m, params[i][:, lanes], states[i][:, lanes])
            store(i, lanes, nxt, new)
            store_half(at, nxt)
    both = []
    for j in range(2):
        m = total[12 * B + j : 12 * B + j + 1, :B] * (1.0 / SCALE_VEC)
        nxt, new = step(m, params[6 + j][...], states[6 + j][...])
        store(6 + j, slice(None), nxt, new)
        both.append(jnp.concatenate([nxt, nxt], axis=1))
    row = lax.broadcasted_iota(jnp.int32, (8, 128), 0)
    n = jnp.broadcast_to(both[0], (8, 128))
    b = jnp.broadcast_to(both[1], (8, 128))
    store_half(12 * B, jnp.where(row == 0, n, jnp.where(row == 1, b, 0.0)))


def halves_kernel(parts, total, *refs):
    half = refs[16]

    def store_half(at, nxt):
        half[at : at + nxt.shape[0], :] = nxt.astype(jnp.bfloat16)

    steps(parts, total, refs[:8], refs[8:16], lambda *_: None, store_half)


def halves(parts, total, params, states):
    return pl.pallas_call(
        halves_kernel,
        in_specs=[VM] * 18,
        out_specs=VM,
        out_shape=pltpu.VMEM((T, 128), jnp.bfloat16),
        compiler_params=PARAMS,
        name="halves",
    )(vmem(parts), vmem(total), *params, *states)


def update_kernel(parts, total, *refs):
    nexts, news = refs[16:24], refs[24:32]

    def store(i, lanes, nxt, new):
        nexts[i][:, lanes] = nxt
        news[i][:, lanes] = new

    steps(parts, total, refs[:8], refs[8:16], store, lambda *_: None)


def update(parts, total, params, states):
    shapes = [jax.ShapeDtypeStruct(p.shape, jnp.float32) for p in params]
    out = pl.pallas_call(
        update_kernel,
        in_specs=[VM] * 18,
        out_shape=(*shapes, *shapes),
        compiler_params=PARAMS,
        name="update",
    )(vmem(parts), vmem(total), *params, *states)
    return out[:8], out[8:]


def unpack_kernel(at_ref, *refs):
    stacks, (up, query, key, value, down, mixed, vectors, *scratch) = refs[:8], refs[8:]
    up_s, query_s, key_s, value_s, down_s, mixed_s, rest_s, sems = scratch
    for n, d in enumerate(ORDER):
        for k, e in enumerate(NEAR):
            s, i = stacks[2 * n + k // 2], k % 2
            r = block_of(at_ref, (at_ref[0] - d) & 3, (at_ref[1] - e) & 3)
            rows = pl.ds(pl.multiple_of(r * B, B), B)
            for c in range(4):
                up_s[rows, c * 128 : c * 128 + 128] = s[i, c * B : c * B + B, :]
            query_s[rows, :] = s[i, 4 * B : 5 * B, :]
            key_s[rows, :] = s[i, 5 * B : 6 * B, :]
            value_s[rows, :] = s[i, 6 * B : 7 * B, :]
            rest_s[pl.ds(r, 1)] = s[i, 7 * B :, :][None]
    pairs = ((up_s, up), (query_s, query), (key_s, key), (value_s, value), (down_s, down), (mixed_s, mixed))
    copies = [pltpu.make_async_copy(a, b, sems.at[k]) for k, (a, b) in enumerate(pairs)]
    for k in range(4):
        copies[k].start()
    lane = lax.broadcasted_iota(jnp.int32, (8, 128), 1)
    for p in range(8):
        lanes = slice(p * 128, p * 128 + 128)
        for k in range(5):
            one = [rest_s[2 * p + j, k * B : k * B + B, :] for j in range(2)]
            tile = jnp.concatenate(one, axis=0).T
            if k < 4:
                down_s[k * 128 : k * 128 + 128, lanes] = tile
            else:
                mixed_s[:, lanes] = tile
        one = [rest_s[2 * p + j, 5 * B :, :].astype(jnp.float32) for j in range(2)]
        last = jnp.where(lane < B, one[0], one[1])
        vectors[p : p + 1, :] = last[0:1]
        vectors[8 + p : 9 + p, :] = last[1:2]
    for k in range(4, 6):
        copies[k].start()
    for c in copies:
        c.wait()


def unpack(place, stacks):
    bf16 = jnp.bfloat16
    shapes = ((1024, 512), (1024, 128), (1024, 128), (1024, 128), (512, 1024), (128, 1024))
    return pl.pallas_call(
        unpack_kernel,
        in_specs=[SM] + [VM] * 8,
        out_specs=(*[HB] * 6, VM),
        out_shape=(*[jax.ShapeDtypeStruct(s, bf16) for s in shapes], pltpu.VMEM((16, 128), jnp.float32)),
        scratch_shapes=[
            *[pltpu.VMEM(s, bf16) for s in shapes],
            pltpu.VMEM((16, 5 * B + 8, 128), bf16),
            pltpu.SemaphoreType.DMA((6,)),
        ],
        compiler_params=PARAMS,
        name="unpack",
    )(place, *[vmem(s) for s in stacks])


def local(*args):
    f16, f32, bf16 = jnp.float16, jnp.float32, jnp.bfloat16
    at = lax.axis_index("replica").astype(jnp.int32)
    core = lax.axis_index("model").astype(jnp.int32) & 1
    zi, yi = at >> 2, at & 3
    place = jnp.stack([jnp.where(core == 0, yi, zi), jnp.where(core == 0, zi, yi), core])

    def inner(xs):
        up, down, query, key, value, mixed, norm, bias = xs
        return up, query, key, value, down, mixed, norm, bias

    def turned(xs):
        up, query, key, value, down, mixed, norm, bias = inner(xs)
        return [vmem(x) for x in (up, query, key, value, down.T, mixed.T, norm[None], bias[None])]

    slopes, params, states = inner(args[:8]), turned(args[8:16]), turned(args[16:24])

    packed_a, packed_b = pack(place, slopes, ORDER[1:])
    two_a, one_a, three_a = [packed_a[o].reshape(CUT, 256) * SCALE for o in range(3)]
    two_b, one_b, three_b = [packed_b[o] * SCALE for o in range(3)]
    out = [x.astype(f16) for x in (two_a, two_b, one_b, three_a)]
    got = [send(x, 0, d) for x, d in zip(out, (1, 3, 1, 3))]
    mid_a = ((one_a + got[0].astype(f32)) * 0.5).astype(f16)
    mid_b = ((three_b + got[1].astype(f32)) * 0.5).astype(f16)
    through = send(mid_a, 0, 1), send(mid_b, 0, 3)
    later = lax.optimization_barrier((place, mid_a, mid_b))[0]
    own_a, own_b = pack(later, slopes, (0,))
    four_a = (own_a.reshape(CUT, 256) * SCALE + got[3].astype(f32) + 2.0 * through[0].astype(f32)) * 0.25
    four_b = (own_b[0] * SCALE + got[2].astype(f32) + 2.0 * through[1].astype(f32)) * 0.25
    four = turn(place, four_a, four_b)
    total = four[0] + sum(send(four[e].astype(f16), 1, e).astype(f32) for e in ORDER[1:])

    part = norms(lax.axis_size("model"), total, *params[:6])
    parts = lax.all_to_all(part, "model", 0, 0, tiled=True)
    half = halves(parts, total, params, states)

    row = [half] + [send(half, 1, e) for e in NEAR[1:]]
    own_a, own_b = jnp.stack(row[:2]), jnp.stack(row[2:])

    def marked(x, d):
        return send(x, 0, d)

    one_a, three_a = marked(own_a, 1), marked(own_a, 3)
    three_b, one_b = marked(own_b, 3), marked(own_b, 1)
    two_a, two_b = marked(one_a, 1), marked(three_b, 3)
    stacks = [own_a, own_b, two_a, two_b, one_a, one_b, three_a, three_b]
    nexts, news = update(lax.optimization_barrier((parts, own_a, own_b))[0], total, params, states)
    up, query, key, value, down, mixed, vectors = unpack(place, stacks)
    vectors = vectors.astype(bf16)
    norm, bias = vectors[:8].reshape(1024), vectors[8:].reshape(1024)

    def outer(xs):
        up, query, key, value, down, mixed, norm, bias = xs
        return up, down.T, query, key, value, mixed.T, norm[0], bias[0]

    return (up, down, query, key, value, mixed, norm, bias, *outer(nexts), *outer(news))


def solution(mesh):
    cut = [P("replica", "model"), P("model", "replica")] + [P("replica", "model")] * 3
    cut += [P("model", "replica"), P("replica"), P("replica")]
    slope = [P("replica", None, "model"), P("replica", "model", None)] + [P("replica", None, "model")] * 3
    slope += [P("replica", "model", None), P("replica", None), P("replica", None)]
    half = [P(None, "model"), P("model", None)] + [P(None, "model")] * 3 + [P("model", None), P(), P()]
    return jax.shard_map(
        local,
        mesh=mesh,
        in_specs=(*slope, *cut, *cut),
        out_specs=(*half, *cut, *cut),
        check_vma=False,
    )
```

profile of v0, /device:TPU:24, one launch (start us, length us, event | category | flops | bytes accessed | tf_op | source)
XLA Modules:
  0.0 80.1 jit_solution(6458418242519092693)
XLA Ops:
  0.7 3.4 %shard_map.415 = (f32[3,4,192,256]{3,2,1,0:T(8,128)S(1)}, f32[3,776,256]{2,1,0:T(8,128)S(1)}) custom-call(s32[3]{0:T(128)S(1)} %pad_add_fusion.at_ref, f32[4,4,64,512]{3,2,1,0:T(8,128)} %bitcast.90, f32[4,4,64,128]{3,2,1,0:T(8,128)} %bitcast.92, f32[4,4,64,128]{3,2,1,0:T(8,128)} %bitcast.94, f32[1024,128]{1,0:T(8,128)} %bitcast.96, f32[1,512,1024]{2,1,0:T(8,128)} %down.3, ...), custom_call_target="tpu_custom_call" | custom-call | tf_op jit(solution)/shard_map/pallas_call | solution.py:138
  4.7 2.0 %collective-permute-start.1 = (f16[776,256]{1,0:T(8,128)(2,1)S(1)}, f16[776,256]{1,0:T(8,128)(2,1)S(1)}, u32[]{:S(2)}, u32[]{:S(2)}) collective-permute-start(f16[776,256]{1,0:T(8,128)(2,1)S(1)} %get-tuple-element.83), channel_id=1, source_target_pairs={{0,24},{1,97},{2,26},{3,99},{4,28},{5,101},{6,30},{7,103},{8,0},{9... | collective-permute-start | bytes 1191944 | tf_op jit(solution)/shard_map/ppermute | solution.py:49
  7.5 2.5 %collective-permute-start.4 = (f16[776,256]{1,0:T(8,128)(2,1)S(1)}, f16[776,256]{1,0:T(8,128)(2,1)S(1)}, u32[]{:S(2)}, u32[]{:S(2)}) collective-permute-start(f16[776,256]{1,0:T(8,128)(2,1)S(1)} %get-tuple-element.82), channel_id=1, source_target_pairs={{0,8},{1,33},{2,10},{3,35},{4,12},{5,37},{6,14},{7,39},{8,16},{9,4... | collective-permute-start | bytes 1191944 | tf_op jit(solution)/shard_map/ppermute | solution.py:49
  10.0 2.3 %collective-permute-done = f16[768,256]{1,0:T(8,128)(2,1)S(1)} collective-permute-done((f16[768,256]{1,0:T(8,128)(2,1)S(1)}, f16[768,256]{1,0:T(8,128)(2,1)S(1)}, u32[]{:S(2)}, u32[]{:S(2)}) %collective-permute-start) | collective-permute-done | bytes 393248 | tf_op jit(solution)/shard_map/ppermute | solution.py:49
  12.4 1.4 %collective-permute-start.3 = (f16[768,256]{1,0:T(8,128)(2,1)S(1)}, f16[768,256]{1,0:T(8,128)(2,1)S(1)}, u32[]{:S(2)}, u32[]{:S(2)}) collective-permute-start(f16[768,256]{1,0:T(8,128)(2,1)S(1)} %fusion.7), channel_id=1, source_target_pairs={{0,8},{1,33},{2,10},{3,35},{4,12},{5,37},{6,14},{7,39},{8,16},{9,4... | collective-permute-start | bytes 1179656 | tf_op jit(solution)/shard_map/ppermute | solution.py:49
  14.8 2.7 %shard_map.416 = (f32[1,4,192,256]{3,2,1,0:T(8,128)S(1)}, f32[1,776,256]{2,1,0:T(8,128)S(1)}) custom-call(s32[3]{0:T(128)S(1)} %pad_add_fusion.at_ref, f32[4,4,64,512]{3,2,1,0:T(8,128)} %bitcast.91, f32[4,4,64,128]{3,2,1,0:T(8,128)} %bitcast.93, f32[4,4,64,128]{3,2,1,0:T(8,128)} %bitcast.95, f32[1024,128]{1,0:T(8,128)} %bitcast.97, f32[1,512,1024]{2,1,0:T(8,128)} %down.3, ...), custom_call_target="tpu_custom_call" | custom-call | tf_op jit(solution)/shard_map/pallas_call | solution.py:138
  18.1 2.6 %collective-permute-done.3 = f16[768,256]{1,0:T(8,128)(2,1)S(1)} collective-permute-done((f16[768,256]{1,0:T(8,128)(2,1)S(1)}, f16[768,256]{1,0:T(8,128)(2,1)S(1)}, u32[]{:S(2)}, u32[]{:S(2)}) %collective-permute-start.3) | collective-permute-done | bytes 393248 | tf_op jit(solution)/shard_map/ppermute | solution.py:49
  20.9 2.2 %collective-permute-done.5 = f16[776,256]{1,0:T(8,128)(2,1)S(1)} collective-permute-done((f16[776,256]{1,0:T(8,128)(2,1)S(1)}, f16[776,256]{1,0:T(8,128)(2,1)S(1)}, u32[]{:S(2)}, u32[]{:S(2)}) %collective-permute-start.5) | collective-permute-done | bytes 397344 | tf_op jit(solution)/shard_map/ppermute | solution.py:49
  24.6 4.2 %collective-permute-start.8 = (f16[776,128]{1,0:T(8,128)(2,1)S(1)}, f16[776,128]{1,0:T(8,128)(2,1)S(1)}, u32[]{:S(2)}, u32[]{:S(2)}) collective-permute-start(f16[776,128]{1,0:T(8,128)(2,1)S(1)} %get-tuple-element.88), channel_id=1, source_target_pairs={{0,96},{1,25},{2,98},{3,27},{4,100},{5,29},{6,102},{7,31},{8,104},... | collective-permute-start | bytes 595976 | tf_op jit(solution)/shard_map/ppermute | solution.py:49
  28.8 1.9 %collective-permute-start.6 = (f16[776,128]{1,0:T(8,128)(2,1)S(1)}, f16[776,128]{1,0:T(8,128)(2,1)S(1)}, u32[]{:S(2)}, u32[]{:S(2)}) collective-permute-start(f16[776,128]{1,0:T(8,128)(2,1)S(1)} %get-tuple-element.87), channel_id=1, source_target_pairs={{0,64},{1,17},{2,66},{3,19},{4,68},{5,21},{6,70},{7,23},{8,72},{9,... | collective-permute-start | bytes 595976 | tf_op jit(solution)/shard_map/ppermute | solution.py:49
  30.7 1.3 %collective-permute-done.8 = f16[776,128]{1,0:T(8,128)(2,1)S(1)} collective-permute-done((f16[776,128]{1,0:T(8,128)(2,1)S(1)}, f16[776,128]{1,0:T(8,128)(2,1)S(1)}, u32[]{:S(2)}, u32[]{:S(2)}) %collective-permute-start.8) | collective-permute-done | bytes 198688 | tf_op jit(solution)/shard_map/ppermute | solution.py:49
  32.0 5.8 %collective-permute-done.7 = f16[776,128]{1,0:T(8,128)(2,1)S(1)} collective-permute-done((f16[776,128]{1,0:T(8,128)(2,1)S(1)}, f16[776,128]{1,0:T(8,128)(2,1)S(1)}, u32[]{:S(2)}, u32[]{:S(2)}) %collective-permute-start.7) | collective-permute-done | bytes 198688 | tf_op jit(solution)/shard_map/ppermute | solution.py:49
  38.2 9.7 %all_to_all.5.parts = f32[8,16,128]{2,1,0:T(8,128)S(1)} all-to-all(f32[8,16,128]{2,1,0:T(8,128)S(1)} %norms.1), channel_id=1, replica_groups=mesh['replica'=16,'model'=8] {'model'}, dimensions={0} | all-to-all | bytes 131072 | tf_op jit(solution)/shard_map/all_to_all | solution.py:380
  48.4 2.8 %collective-permute-start.11 = (bf16[776,128]{1,0:T(8,128)(2,1)S(1)}, bf16[776,128]{1,0:T(8,128)(2,1)S(1)}, u32[]{:S(2)}, u32[]{:S(2)}) collective-permute-start(bf16[776,128]{1,0:T(8,128)(2,1)S(1)} %halves.1), channel_id=1, source_target_pairs={{0,64},{1,17},{2,66},{3,19},{4,68},{5,21},{6,70},{7,23},{8,72},{9,... | collective-permute-start | bytes 595976 | tf_op jit(solution)/shard_map/ppermute | solution.py:49
  51.7 6.1 %collective-permute-done.9 = bf16[776,128]{1,0:T(8,128)(2,1)S(1)} collective-permute-done((bf16[776,128]{1,0:T(8,128)(2,1)S(1)}, bf16[776,128]{1,0:T(8,128)(2,1)S(1)}, u32[]{:S(2)}, u32[]{:S(2)}) %collective-permute-start.9) | collective-permute-done | bytes 198688 | tf_op jit(solution)/shard_map/ppermute | solution.py:49
  58.4 1.6 %collective-permute-start.14 = (bf16[2,776,128]{2,1,0:T(8,128)(2,1)S(1)}, bf16[2,776,128]{2,1,0:T(8,128)(2,1)S(1)}, u32[]{:S(2)}, u32[]{:S(2)}) collective-permute-start(bf16[2,776,128]{2,1,0:T(8,128)(2,1)S(1)} %pad_maximum_fusion.1.refs_1_), channel_id=1, source_target_pairs={{0,24},{1,97},{2,26},{3,99},{4,28},{5,101},{6,30},{7,103},{8,0},{9... | collective-permute-start | bytes 1191944 | tf_op jit(solution)/shard_map/ppermute | solution.py:49
  60.0 1.7 %collective-permute-start.16 = (bf16[2,776,128]{2,1,0:T(8,128)(2,1)S(1)}, bf16[2,776,128]{2,1,0:T(8,128)(2,1)S(1)}, u32[]{:S(2)}, u32[]{:S(2)}) collective-permute-start(bf16[2,776,128]{2,1,0:T(8,128)(2,1)S(1)} %pad_maximum_fusion.1.refs_1_), channel_id=1, source_target_pairs={{0,8},{1,33},{2,10},{3,35},{4,12},{5,37},{6,14},{7,39},{8,16},{9,4... | collective-permute-start | bytes 1191944 | tf_op jit(solution)/shard_map/ppermute | solution.py:49
  62.0 3.6 %collective-permute-done.12.refs_4_ = bf16[2,776,128]{2,1,0:T(8,128)(2,1)S(1)} collective-permute-done((bf16[2,776,128]{2,1,0:T(8,128)(2,1)S(1)}, bf16[2,776,128]{2,1,0:T(8,128)(2,1)S(1)}, u32[]{:S(2)}, u32[]{:S(2)}) %collective-permute-start.12) | collective-permute-done | bytes 397344 | tf_op jit(solution)/shard_map/ppermute | solution.py:49
  65.7 1.2 %collective-permute-start.13 = (bf16[2,776,128]{2,1,0:T(8,128)(2,1)S(1)}, bf16[2,776,128]{2,1,0:T(8,128)(2,1)S(1)}, u32[]{:S(2)}, u32[]{:S(2)}) collective-permute-start(bf16[2,776,128]{2,1,0:T(8,128)(2,1)S(1)} %collective-permute-done.12.refs_4_), channel_id=1, source_target_pairs={{0,8},{1,33},{2,10},{3,35},{4,12},{5,37},{6,14},{7,39},{8,16},{9,4... | collective-permute-start | bytes 1191944 | tf_op jit(solution)/shard_map/ppermute | solution.py:49
  67.8 1.2 %update.1 = (f32[64,512]{1,0:T(8,128)}, f32[64,128]{1,0:T(8,128)}, f32[64,128]{1,0:T(8,128)}, f32[64,128]{1,0:T(8,128)}, f32[64,512]{1,0:T(8,128)}, /*index=5*/f...) custom-call(f32[8,16,128]{2,1,0:T(8,128)S(1)} %all_to_all.5.parts, ...), custom_call_target="tpu_custom_call" | custom-call | tf_op jit(solution)/shard_map/update/pallas_call | solution.py:281
  69.9 1.8 %collective-permute-done.17.refs_6_ = bf16[2,776,128]{2,1,0:T(8,128)(2,1)S(1)} collective-permute-done((bf16[2,776,128]{2,1,0:T(8,128)(2,1)S(1)}, bf16[2,776,128]{2,1,0:T(8,128)(2,1)S(1)}, u32[]{:S(2)}, u32[]{:S(2)}) %collective-permute-start.17) | collective-permute-done | bytes 397344 | tf_op jit(solution)/shard_map/ppermute | solution.py:49
  71.8 2.4 %collective-permute-done.13.refs_2_ = bf16[2,776,128]{2,1,0:T(8,128)(2,1)S(1)} collective-permute-done((bf16[2,776,128]{2,1,0:T(8,128)(2,1)S(1)}, bf16[2,776,128]{2,1,0:T(8,128)(2,1)S(1)}, u32[]{:S(2)}, u32[]{:S(2)}) %collective-permute-start.13) | collective-permute-done | bytes 397344 | tf_op jit(solution)/shard_map/ppermute | solution.py:49
  74.2 2.4 %collective-permute-done.15.refs_3_ = bf16[2,776,128]{2,1,0:T(8,128)(2,1)S(1)} collective-permute-done((bf16[2,776,128]{2,1,0:T(8,128)(2,1)S(1)}, bf16[2,776,128]{2,1,0:T(8,128)(2,1)S(1)}, u32[]{:S(2)}, u32[]{:S(2)}) %collective-permute-start.15) | collective-permute-done | bytes 397344 | tf_op jit(solution)/shard_map/ppermute | solution.py:49
  76.5 2.9 %unpack.1 = (bf16[1024,512]{1,0:T(8,128)(2,1)}, bf16[1024,128]{1,0:T(8,128)(2,1)}, bf16[1024,128]{1,0:T(8,128)(2,1)}, bf16[1024,128]{1,0:T(8,128)(2,1)}, bf16[51...) custom-call(s32[3]{0:T(128)S(1)} %pad_add_fusion.at_ref, ...), custom_call_target="tpu_custom_call" | custom-call | tf_op jit(solution)/shard_map/unpack/pallas_call | solution.py:332
  (67 shorter events, 9.2 us)
Async XLA Ops:
  4.4 7.8 %collective-permute-start = (f16[768,256]{1,0:T(8,128)(2,1)S(1)}, f16[768,256]{1,0:T(8,128)(2,1)S(1)}, u32[]{:S(2)}, u32[]{:S(2)}) collective-permute-start(f16[768,256]{1,0:T(8,128)(2,1)S(1)} %bitcast.99), channel_id=1, source_target_pairs={{0,8},{1,33},{2,10},{3,35},{4,12},{5,37},{6,14},{7,39},{8,16},{9,4... | collective-permute-start | bytes 1179656 | tf_op jit(solution)/shard_map/ppermute | solution.py:49
  4.7 9.1 %collective-permute-start.1 = (f16[776,256]{1,0:T(8,128)(2,1)S(1)}, f16[776,256]{1,0:T(8,128)(2,1)S(1)}, u32[]{:S(2)}, u32[]{:S(2)}) collective-permute-start(f16[776,256]{1,0:T(8,128)(2,1)S(1)} %get-tuple-element.83), channel_id=1, source_target_pairs={{0,24},{1,97},{2,26},{3,99},{4,28},{5,101},{6,30},{7,103},{8,0},{9... | collective-permute-start | bytes 1191944 | tf_op jit(solution)/shard_map/ppermute | solution.py:49
  6.7 11.3 %collective-permute-start.2 = (f16[768,256]{1,0:T(8,128)(2,1)S(1)}, f16[768,256]{1,0:T(8,128)(2,1)S(1)}, u32[]{:S(2)}, u32[]{:S(2)}) collective-permute-start(f16[768,256]{1,0:T(8,128)(2,1)S(1)} %bitcast.98), channel_id=1, source_target_pairs={{0,24},{1,97},{2,26},{3,99},{4,28},{5,101},{6,30},{7,103},{8,0},{9... | collective-permute-start | bytes 1179656 | tf_op jit(solution)/shard_map/ppermute | solution.py:49
  7.5 13.4 %collective-permute-start.4 = (f16[776,256]{1,0:T(8,128)(2,1)S(1)}, f16[776,256]{1,0:T(8,128)(2,1)S(1)}, u32[]{:S(2)}, u32[]{:S(2)}) collective-permute-start(f16[776,256]{1,0:T(8,128)(2,1)S(1)} %get-tuple-element.82), channel_id=1, source_target_pairs={{0,8},{1,33},{2,10},{3,35},{4,12},{5,37},{6,14},{7,39},{8,16},{9,4... | collective-permute-start | bytes 1191944 | tf_op jit(solution)/shard_map/ppermute | solution.py:49
  12.4 8.3 %collective-permute-start.3 = (f16[768,256]{1,0:T(8,128)(2,1)S(1)}, f16[768,256]{1,0:T(8,128)(2,1)S(1)}, u32[]{:S(2)}, u32[]{:S(2)}) collective-permute-start(f16[768,256]{1,0:T(8,128)(2,1)S(1)} %fusion.7), channel_id=1, source_target_pairs={{0,8},{1,33},{2,10},{3,35},{4,12},{5,37},{6,14},{7,39},{8,16},{9,4... | collective-permute-start | bytes 1179656 | tf_op jit(solution)/shard_map/ppermute | solution.py:49
  14.0 9.1 %collective-permute-start.5 = (f16[776,256]{1,0:T(8,128)(2,1)S(1)}, f16[776,256]{1,0:T(8,128)(2,1)S(1)}, u32[]{:S(2)}, u32[]{:S(2)}) collective-permute-start(f16[776,256]{1,0:T(8,128)(2,1)S(1)} %fusion.3), channel_id=1, source_target_pairs={{0,24},{1,97},{2,26},{3,99},{4,28},{5,101},{6,30},{7,103},{8,0},{9... | collective-permute-start | bytes 1191944 | tf_op jit(solution)/shard_map/ppermute | solution.py:49
  24.3 23.6 %copy-start.2 = (f32[64,512]{1,0:T(8,128)S(1)}, f32[64,512]{1,0:T(8,128)}, u32[]{:S(2)}) copy-start(f32[64,512]{1,0:T(8,128)} %refs_8_.3) | copy-start | bytes 393220
  24.3 23.6 %copy-start.3 = (f32[512,64]{0,1:T(8,128)S(1)}, f32[512,64]{0,1:T(8,128)}, u32[]{:S(2)}) copy-start(f32[512,64]{0,1:T(8,128)} %param.41) | copy-start | bytes 393220
  24.4 23.6 %copy-start.8 = (f32[64,128]{1,0:T(8,128)S(1)}, f32[64,128]{1,0:T(8,128)}, u32[]{:S(2)}) copy-start(f32[64,128]{1,0:T(8,128)} %refs_9_.3) | copy-start | bytes 98308
  24.4 23.6 %copy-start.9 = (f32[64,128]{1,0:T(8,128)S(1)}, f32[64,128]{1,0:T(8,128)}, u32[]{:S(2)}) copy-start(f32[64,128]{1,0:T(8,128)} %refs_10_.3) | copy-start | bytes 98308
  24.4 23.6 %copy-start.10 = (f32[64,128]{1,0:T(8,128)S(1)}, f32[64,128]{1,0:T(8,128)}, u32[]{:S(2)}) copy-start(f32[64,128]{1,0:T(8,128)} %refs_11_.3) | copy-start | bytes 98308
  24.4 23.6 %copy-start.11 = (f32[128,64]{0,1:T(8,128)S(1)}, f32[128,64]{0,1:T(8,128)}, u32[]{:S(2)}) copy-start(f32[128,64]{0,1:T(8,128)} %param.45) | copy-start | bytes 98308
  24.6 7.4 %collective-permute-start.8 = (f16[776,128]{1,0:T(8,128)(2,1)S(1)}, f16[776,128]{1,0:T(8,128)(2,1)S(1)}, u32[]{:S(2)}, u32[]{:S(2)}) collective-permute-start(f16[776,128]{1,0:T(8,128)(2,1)S(1)} %get-tuple-element.88), channel_id=1, source_target_pairs={{0,96},{1,25},{2,98},{3,27},{4,100},{5,29},{6,102},{7,31},{8,104},... | collective-permute-start | bytes 595976 | tf_op jit(solution)/shard_map/ppermute | solution.py:49
  28.8 9.0 %collective-permute-start.7 = (f16[776,128]{1,0:T(8,128)(2,1)S(1)}, f16[776,128]{1,0:T(8,128)(2,1)S(1)}, u32[]{:S(2)}, u32[]{:S(2)}) collective-permute-start(f16[776,128]{1,0:T(8,128)(2,1)S(1)} %get-tuple-element.89), channel_id=1, source_target_pairs={{0,32},{1,9},{2,34},{3,11},{4,36},{5,13},{6,38},{7,15},{8,40},{9,1... | collective-permute-start | bytes 595976 | tf_op jit(solution)/shard_map/ppermute | solution.py:49
  28.8 9.0 %collective-permute-start.6 = (f16[776,128]{1,0:T(8,128)(2,1)S(1)}, f16[776,128]{1,0:T(8,128)(2,1)S(1)}, u32[]{:S(2)}, u32[]{:S(2)}) collective-permute-start(f16[776,128]{1,0:T(8,128)(2,1)S(1)} %get-tuple-element.87), channel_id=1, source_target_pairs={{0,64},{1,17},{2,66},{3,19},{4,68},{5,21},{6,70},{7,23},{8,72},{9,... | collective-permute-start | bytes 595976 | tf_op jit(solution)/shard_map/ppermute | solution.py:49
  48.4 9.4 %collective-permute-start.9 = (bf16[776,128]{1,0:T(8,128)(2,1)S(1)}, bf16[776,128]{1,0:T(8,128)(2,1)S(1)}, u32[]{:S(2)}, u32[]{:S(2)}) collective-permute-start(bf16[776,128]{1,0:T(8,128)(2,1)S(1)} %halves.1), channel_id=1, source_target_pairs={{0,32},{1,9},{2,34},{3,11},{4,36},{5,13},{6,38},{7,15},{8,40},{9,1... | collective-permute-start | bytes 595976 | tf_op jit(solution)/shard_map/ppermute | solution.py:49
  48.4 9.4 %collective-permute-start.11 = (bf16[776,128]{1,0:T(8,128)(2,1)S(1)}, bf16[776,128]{1,0:T(8,128)(2,1)S(1)}, u32[]{:S(2)}, u32[]{:S(2)}) collective-permute-start(bf16[776,128]{1,0:T(8,128)(2,1)S(1)} %halves.1), channel_id=1, source_target_pairs={{0,64},{1,17},{2,66},{3,19},{4,68},{5,21},{6,70},{7,23},{8,72},{9,... | collective-permute-start | bytes 595976 | tf_op jit(solution)/shard_map/ppermute | solution.py:49
  51.3 7.1 %collective-permute-start.10 = (bf16[776,128]{1,0:T(8,128)(2,1)S(1)}, bf16[776,128]{1,0:T(8,128)(2,1)S(1)}, u32[]{:S(2)}, u32[]{:S(2)}) collective-permute-start(bf16[776,128]{1,0:T(8,128)(2,1)S(1)} %halves.1), channel_id=1, source_target_pairs={{0,96},{1,25},{2,98},{3,27},{4,100},{5,29},{6,102},{7,31},{8,104},... | collective-permute-start | bytes 595976 | tf_op jit(solution)/shard_map/ppermute | solution.py:49
  57.8 7.9 %collective-permute-start.12 = (bf16[2,776,128]{2,1,0:T(8,128)(2,1)S(1)}, bf16[2,776,128]{2,1,0:T(8,128)(2,1)S(1)}, u32[]{:S(2)}, u32[]{:S(2)}) collective-permute-start(bf16[2,776,128]{2,1,0:T(8,128)(2,1)S(1)} %pad_maximum_fusion.refs_0_), channel_id=1, source_target_pairs={{0,8},{1,33},{2,10},{3,35},{4,12},{5,37},{6,14},{7,39},{8,16},{9,4... | collective-permute-start | bytes 1191944 | tf_op jit(solution)/shard_map/ppermute | solution.py:49
  58.4 9.1 %collective-permute-start.14 = (bf16[2,776,128]{2,1,0:T(8,128)(2,1)S(1)}, bf16[2,776,128]{2,1,0:T(8,128)(2,1)S(1)}, u32[]{:S(2)}, u32[]{:S(2)}) collective-permute-start(bf16[2,776,128]{2,1,0:T(8,128)(2,1)S(1)} %pad_maximum_fusion.1.refs_1_), channel_id=1, source_target_pairs={{0,24},{1,97},{2,26},{3,99},{4,28},{5,101},{6,30},{7,103},{8,0},{9... | collective-permute-start | bytes 1191944 | tf_op jit(solution)/shard_map/ppermute | solution.py:49
  60.0 9.9 %collective-permute-start.16 = (bf16[2,776,128]{2,1,0:T(8,128)(2,1)S(1)}, bf16[2,776,128]{2,1,0:T(8,128)(2,1)S(1)}, u32[]{:S(2)}, u32[]{:S(2)}) collective-permute-start(bf16[2,776,128]{2,1,0:T(8,128)(2,1)S(1)} %pad_maximum_fusion.1.refs_1_), channel_id=1, source_target_pairs={{0,8},{1,33},{2,10},{3,35},{4,12},{5,37},{6,14},{7,39},{8,16},{9,4... | collective-permute-start | bytes 1191944 | tf_op jit(solution)/shard_map/ppermute | solution.py:49
  61.7 10.1 %collective-permute-start.17 = (bf16[2,776,128]{2,1,0:T(8,128)(2,1)S(1)}, bf16[2,776,128]{2,1,0:T(8,128)(2,1)S(1)}, u32[]{:S(2)}, u32[]{:S(2)}) collective-permute-start(bf16[2,776,128]{2,1,0:T(8,128)(2,1)S(1)} %pad_maximum_fusion.refs_0_), channel_id=1, source_target_pairs={{0,24},{1,97},{2,26},{3,99},{4,28},{5,101},{6,30},{7,103},{8,0},{9... | collective-permute-start | bytes 1191944 | tf_op jit(solution)/shard_map/ppermute | solution.py:49
  65.7 8.5 %collective-permute-start.13 = (bf16[2,776,128]{2,1,0:T(8,128)(2,1)S(1)}, bf16[2,776,128]{2,1,0:T(8,128)(2,1)S(1)}, u32[]{:S(2)}, u32[]{:S(2)}) collective-permute-start(bf16[2,776,128]{2,1,0:T(8,128)(2,1)S(1)} %collective-permute-done.12.refs_4_), channel_id=1, source_target_pairs={{0,8},{1,33},{2,10},{3,35},{4,12},{5,37},{6,14},{7,39},{8,16},{9,4... | collective-permute-start | bytes 1191944 | tf_op jit(solution)/shard_map/ppermute | solution.py:49
  67.5 9.0 %collective-permute-start.15 = (bf16[2,776,128]{2,1,0:T(8,128)(2,1)S(1)}, bf16[2,776,128]{2,1,0:T(8,128)(2,1)S(1)}, u32[]{:S(2)}, u32[]{:S(2)}) collective-permute-start(bf16[2,776,128]{2,1,0:T(8,128)(2,1)S(1)} %collective-permute-done.14.refs_7_), channel_id=1, source_target_pairs={{0,24},{1,97},{2,26},{3,99},{4,28},{5,101},{6,30},{7,103},{8,0},{9... | collective-permute-start | bytes 1191944 | tf_op jit(solution)/shard_map/ppermute | solution.py:49
  (10 other events, 177.1 us)
where the time goes:
time: 80.2 us; the launch traced here: 80.1 us
  waiting for transfers between devices  33.3 us (42%)
  starting transfers between devices  22.2 us (28%)
  Pallas kernels  11.5 us (14%)
  blocking collectives  9.71 us (12%)
  other arithmetic  1.54 us (2%)
  between operations  1.06 us (1%)
  local copies, waits for them, and re-layouts  0.81 us (1%)
    ppermute x18, waiting for transfers between devices, send(): return lax.ppermute(x, ('replica', 'model'), pairs)  33.3 us
    ppermute x18, starting transfers between devices, send(): return lax.ppermute(x, ('replica', 'model'), pairs)  22.2 us
    all_to_all x1, blocking collectives, local(): parts = lax.all_to_all(part, 'model', 0, 0, tiled=True)  9.71 us
    pallas_call x2, Pallas kernels, pack(): pl.pallas_call(kernel, in_specs=[SM] + [HB] * 8, out_specs=(VM, VM), out_...  6.04 us
    pallas_call x1, Pallas kernels, unpack(): pl.pallas_call(unpack_kernel, in_specs=[SM] + [VM] * 8, out_specs=(*[HB]...  2.92 us
  transfers between devices with their start and end apart: 18, of which 15 were waited for; matrix products, arithmetic and copies ran while one was open for 1% of the time, Pallas kernels for 5%

commit v1 on v0

--- a/solution.py
+++ b/solution.py
@@ -21,7 +21,6 @@
 SCALE = 8192.0
 SCALE_VEC = 4096.0
 ORDER = (0, 2, 1, 3)
-NEAR = (0, 1, 3, 2)
 
 
 def vmem(x):
@@ -47,6 +46,10 @@
                 to = (z * 4 + (y + d) % 4) if along_y else ((z + d) % 4 * 4 + y)
                 pairs.append(((z * 4 + y) * 8 + m, to * 8 + m))
     return lax.ppermute(x, ("replica", "model"), pairs)
+
+
+def marked(x, d, stage=1):
+    return send(x, stage, d)
 
 
 def block_of(at_ref, f, s):
@@ -199,25 +202,22 @@
         table = jnp.where(lane == m, o, jnp.where(lane == 8 + m, s, table))
     table = jnp.concatenate([table, jnp.zeros((128 - B, 128), jnp.float32)], axis=0)
     table = table.T[:16, :]
-    for r in range(part.shape[0]):
-        part[r] = table
-
-
-def norms(copies, total, *params):
+    part[...] = table
+
+
+def norms(total, *params):
     return pl.pallas_call(
         norms_kernel,
         in_specs=[VM] * 7,
         out_specs=VM,
-        out_shape=pltpu.VMEM((copies, 16, 128), jnp.float32),
+        out_shape=pltpu.VMEM((16, 128), jnp.float32),
         compiler_params=PARAMS,
         name="norms",
     )(vmem(total), *params)
 
 
 def steps(parts, total, params, states, store, store_half):
-    sums = parts[0]
-    for d in range(1, parts.shape[0]):
-        sums = sums + parts[d]
+    sums = parts[...]
     ratio = jnp.sqrt(sums[:8]) * lax.rsqrt(sums[8:16] + 1e-06)
     ratio = jnp.concatenate([ratio, jnp.zeros((120, 128), jnp.float32)], axis=0).T[:B, :]
 
@@ -292,7 +292,7 @@
     stacks, (up, query, key, value, down, mixed, vectors, *scratch) = refs[:8], refs[8:]
     up_s, query_s, key_s, value_s, down_s, mixed_s, rest_s, sems = scratch
     for n, d in enumerate(ORDER):
-        for k, e in enumerate(NEAR):
+        for k, e in enumerate(ORDER):
             s, i = stacks[2 * n + k // 2], k % 2
             r = block_of(at_ref, (at_ref[0] - d) & 3, (at_ref[1] - e) & 3)
             rows = pl.ds(pl.multiple_of(r * B, B), B)
@@ -374,21 +374,18 @@
     four_a = (own_a.reshape(CUT, 256) * SCALE + got[3].astype(f32) + 2.0 * through[0].astype(f32)) * 0.25
     four_b = (own_b[0] * SCALE + got[2].astype(f32) + 2.0 * through[1].astype(f32)) * 0.25
     four = turn(place, four_a, four_b)
-    total = four[0] + sum(send(four[e].astype(f16), 1, e).astype(f32) for e in ORDER[1:])
-
-    part = norms(lax.axis_size("model"), total, *params[:6])
-    parts = lax.all_to_all(part, "model", 0, 0, tiled=True)
+    total = four[0] + sum(marked(four[e].astype(f16), e).astype(f32) for e in ORDER[1:])
+
+    parts = norms(total, *params[:6])
+    for partner in (lambda m: m ^ 1, lambda m: m ^ 2, lambda m: m ^ 6):
+        parts = parts + lax.ppermute(parts, "model", [(m, partner(m)) for m in range(8)])
     half = halves(parts, total, params, states)
 
-    row = [half] + [send(half, 1, e) for e in NEAR[1:]]
+    row = [half] + [marked(half, e) for e in ORDER[1:]]
     own_a, own_b = jnp.stack(row[:2]), jnp.stack(row[2:])
-
-    def marked(x, d):
-        return send(x, 0, d)
-
-    one_a, three_a = marked(own_a, 1), marked(own_a, 3)
-    three_b, one_b = marked(own_b, 3), marked(own_b, 1)
-    two_a, two_b = marked(one_a, 1), marked(three_b, 3)
+    one_a, three_a = marked(own_a, 1, 0), marked(own_a, 3, 0)
+    three_b, one_b = marked(own_b, 3, 0), marked(own_b, 1, 0)
+    two_a, two_b = send(one_a, 0, 1), send(three_b, 0, 3)
     stacks = [own_a, own_b, two_a, two_b, one_a, one_b, three_a, three_b]
     nexts, news = update(lax.optimization_barrier((parts, own_a, own_b))[0], total, params, states)
     up, query, key, value, down, mixed, vectors = unpack(place, stacks)

time: 80.2 us -> 81 us (level)
  blocking collectives: 9.71 us -> 0 us
  waiting for transfers between devices: 33.3 us -> 40 us
  starting transfers between devices: 22.2 us -> 26 us
    all_to_all x1 -> x0, blocking collectives: 9.71 us -> none  [local(): parts = lax.all_to_all(part, 'model', 0, 0, tiled=True)]
    ppermute x0 -> x3, waiting for transfers between devices: none -> 5.42 us  [local(): lax.ppermute(parts, 'model', [(m, partner(m)) for m in range(8)])]
    ppermute x0 -> x3, starting transfers between devices: none -> 4.29 us  [local(): lax.ppermute(parts, 'model', [(m, partner(m)) for m in range(8)])]
    ppermute x18, waiting for transfers between devices: 33.3 us -> 34.5 us  [send(): return lax.ppermute(x, ('replica', 'model'), pairs)]
  transfers between devices with their start and end apart: 18 -> 21, of which waited for: 15 -> 17; matrix products, arithmetic and copies ran while one was open for 1% -> 1% of each run, Pallas kernels for 5% -> 5%
where the time goes in v1:
time: 81 us; the launch traced here: 80.9 us
  waiting for transfers between devices  40 us (49%)
  starting transfers between devices  26 us (32%)
  Pallas kernels  11.5 us (14%)
  other arithmetic  1.55 us (2%)
  between operations  1.06 us (1%)
  local copies, waits for them, and re-layouts  0.81 us (1%)
    ppermute x18, waiting for transfers between devices, send(): return lax.ppermute(x, ('replica', 'model'), pairs)  34.5 us
    ppermute x18, starting transfers between devices, send(): return lax.ppermute(x, ('replica', 'model'), pairs)  21.7 us
    pallas_call x2, Pallas kernels, pack(): pl.pallas_call(kernel, in_specs=[SM] + [HB] * 8, out_specs=(VM, VM), out_...  6.04 us
    ppermute x3, waiting for transfers between devices, local(): lax.ppermute(parts, 'model', [(m, partner(m)) for m in range(8)])  5.42 us
    ppermute x3, starting transfers between devices, local(): lax.ppermute(parts, 'model', [(m, partner(m)) for m in range(8)])  4.29 us
    pallas_call x1, Pallas kernels, unpack(): pl.pallas_call(unpack_kernel, in_specs=[SM] + [VM] * 8, out_specs=(*[HB]...  2.92 us
  transfers between devices with their start and end apart: 21, of which 17 were waited for; matrix products, arithmetic and copies ran while one was open for 1% of the time, Pallas kernels for 5%

profile of v1, /device:TPU:24, one launch (start us, length us, event | category | flops | bytes accessed | tf_op | source)
XLA Modules:
  0.0 80.9 jit_solution(1264625663478695694)
XLA Ops:
  0.7 3.4 %shard_map.415 = (f32[3,4,192,256]{3,2,1,0:T(8,128)S(1)}, f32[3,776,256]{2,1,0:T(8,128)S(1)}) custom-call(s32[3]{0:T(128)S(1)} %pad_add_fusion.at_ref, f32[4,4,64,512]{3,2,1,0:T(8,128)} %bitcast.90, f32[4,4,64,128]{3,2,1,0:T(8,128)} %bitcast.92, f32[4,4,64,128]{3,2,1,0:T(8,128)} %bitcast.94, f32[1024,128]{1,0:T(8,128)} %bitcast.96, f32[1,512,1024]{2,1,0:T(8,128)} %down.3, ...), custom_call_target="tpu_custom_call" | custom-call | tf_op jit(solution)/shard_map/pallas_call | solution.py:141
  4.8 2.0 %collective-permute-start.1 = (f16[776,256]{1,0:T(8,128)(2,1)S(1)}, f16[776,256]{1,0:T(8,128)(2,1)S(1)}, u32[]{:S(2)}, u32[]{:S(2)}) collective-permute-start(f16[776,256]{1,0:T(8,128)(2,1)S(1)} %get-tuple-element.83), channel_id=1, source_target_pairs={{0,24},{1,97},{2,26},{3,99},{4,28},{5,101},{6,30},{7,103},{8,0},{9... | collective-permute-start | bytes 1191944 | tf_op jit(solution)/shard_map/ppermute | solution.py:48
  7.5 2.5 %collective-permute-start.4 = (f16[776,256]{1,0:T(8,128)(2,1)S(1)}, f16[776,256]{1,0:T(8,128)(2,1)S(1)}, u32[]{:S(2)}, u32[]{:S(2)}) collective-permute-start(f16[776,256]{1,0:T(8,128)(2,1)S(1)} %get-tuple-element.82), channel_id=1, source_target_pairs={{0,8},{1,33},{2,10},{3,35},{4,12},{5,37},{6,14},{7,39},{8,16},{9,4... | collective-permute-start | bytes 1191944 | tf_op jit(solution)/shard_map/ppermute | solution.py:48
  10.0 2.3 %collective-permute-done = f16[768,256]{1,0:T(8,128)(2,1)S(1)} collective-permute-done((f16[768,256]{1,0:T(8,128)(2,1)S(1)}, f16[768,256]{1,0:T(8,128)(2,1)S(1)}, u32[]{:S(2)}, u32[]{:S(2)}) %collective-permute-start) | collective-permute-done | bytes 393248 | tf_op jit(solution)/shard_map/ppermute | solution.py:48
  12.4 1.4 %collective-permute-start.3 = (f16[768,256]{1,0:T(8,128)(2,1)S(1)}, f16[768,256]{1,0:T(8,128)(2,1)S(1)}, u32[]{:S(2)}, u32[]{:S(2)}) collective-permute-start(f16[768,256]{1,0:T(8,128)(2,1)S(1)} %fusion.7), channel_id=1, source_target_pairs={{0,8},{1,33},{2,10},{3,35},{4,12},{5,37},{6,14},{7,39},{8,16},{9,4... | collective-permute-start | bytes 1179656 | tf_op jit(solution)/shard_map/ppermute | solution.py:48
  14.8 2.7 %shard_map.416 = (f32[1,4,192,256]{3,2,1,0:T(8,128)S(1)}, f32[1,776,256]{2,1,0:T(8,128)S(1)}) custom-call(s32[3]{0:T(128)S(1)} %pad_add_fusion.at_ref, f32[4,4,64,512]{3,2,1,0:T(8,128)} %bitcast.91, f32[4,4,64,128]{3,2,1,0:T(8,128)} %bitcast.93, f32[4,4,64,128]{3,2,1,0:T(8,128)} %bitcast.95, f32[1024,128]{1,0:T(8,128)} %bitcast.97, f32[1,512,1024]{2,1,0:T(8,128)} %down.3, ...), custom_call_target="tpu_custom_call" | custom-call | tf_op jit(solution)/shard_map/pallas_call | solution.py:141
  18.1 2.6 %collective-permute-done.3 = f16[768,256]{1,0:T(8,128)(2,1)S(1)} collective-permute-done((f16[768,256]{1,0:T(8,128)(2,1)S(1)}, f16[768,256]{1,0:T(8,128)(2,1)S(1)}, u32[]{:S(2)}, u32[]{:S(2)}) %collective-permute-start.3) | collective-permute-done | bytes 393248 | tf_op jit(solution)/shard_map/ppermute | solution.py:48
  20.9 2.2 %collective-permute-done.5 = f16[776,256]{1,0:T(8,128)(2,1)S(1)} collective-permute-done((f16[776,256]{1,0:T(8,128)(2,1)S(1)}, f16[776,256]{1,0:T(8,128)(2,1)S(1)}, u32[]{:S(2)}, u32[]{:S(2)}) %collective-permute-start.5) | collective-permute-done | bytes 397344 | tf_op jit(solution)/shard_map/ppermute | solution.py:48
  24.6 4.2 %collective-permute-start.8 = (f16[776,128]{1,0:T(8,128)(2,1)S(1)}, f16[776,128]{1,0:T(8,128)(2,1)S(1)}, u32[]{:S(2)}, u32[]{:S(2)}) collective-permute-start(f16[776,128]{1,0:T(8,128)(2,1)S(1)} %get-tuple-element.88), channel_id=1, source_target_pairs={{0,96},{1,25},{2,98},{3,27},{4,100},{5,29},{6,102},{7,31},{8,104},... | collective-permute-start | bytes 595976 | tf_op jit(solution)/shard_map/ppermute | solution.py:48
  28.8 1.9 %collective-permute-start.6 = (f16[776,128]{1,0:T(8,128)(2,1)S(1)}, f16[776,128]{1,0:T(8,128)(2,1)S(1)}, u32[]{:S(2)}, u32[]{:S(2)}) collective-permute-start(f16[776,128]{1,0:T(8,128)(2,1)S(1)} %get-tuple-element.87), channel_id=1, source_target_pairs={{0,64},{1,17},{2,66},{3,19},{4,68},{5,21},{6,70},{7,23},{8,72},{9,... | collective-permute-start | bytes 595976 | tf_op jit(solution)/shard_map/ppermute | solution.py:48
  30.7 1.3 %collective-permute-done.8 = f16[776,128]{1,0:T(8,128)(2,1)S(1)} collective-permute-done((f16[776,128]{1,0:T(8,128)(2,1)S(1)}, f16[776,128]{1,0:T(8,128)(2,1)S(1)}, u32[]{:S(2)}, u32[]{:S(2)}) %collective-permute-start.8) | collective-permute-done | bytes 198688 | tf_op jit(solution)/shard_map/ppermute | solution.py:48
  32.0 5.8 %collective-permute-done.7 = f16[776,128]{1,0:T(8,128)(2,1)S(1)} collective-permute-done((f16[776,128]{1,0:T(8,128)(2,1)S(1)}, f16[776,128]{1,0:T(8,128)(2,1)S(1)}, u32[]{:S(2)}, u32[]{:S(2)}) %collective-permute-start.7) | collective-permute-done | bytes 198688 | tf_op jit(solution)/shard_map/ppermute | solution.py:48
  39.5 1.5 %collective-permute-start.10 = (f32[16,128]{1,0:T(8,128)S(1)}, f32[16,128]{1,0:T(8,128)S(1)}, u32[]{:S(2)}, u32[]{:S(2)}) collective-permute-start(f32[16,128]{1,0:T(8,128)S(1)} %add.45), channel_id=1, source_target_pairs={{0,2},{1,3},{2,0},{3,1},{4,6},{5,7},{6,4},{7,5},{8,10},{9,11},{10,... | collective-permute-start | bytes 24584 | tf_op jit(solution)/shard_map/ppermute | solution.py:381
  41.0 2.2 %collective-permute-done.10 = f32[16,128]{1,0:T(8,128)S(1)} collective-permute-done((f32[16,128]{1,0:T(8,128)S(1)}, f32[16,128]{1,0:T(8,128)S(1)}, u32[]{:S(2)}, u32[]{:S(2)}) %collective-permute-start.10) | collective-permute-done | bytes 8224 | tf_op jit(solution)/shard_map/ppermute | solution.py:381
  43.1 2.8 %collective-permute-start.11 = (f32[16,128]{1,0:T(8,128)S(1)}, f32[16,128]{1,0:T(8,128)S(1)}, u32[]{:S(2)}, u32[]{:S(2)}) collective-permute-start(f32[16,128]{1,0:T(8,128)S(1)} %add.46), channel_id=1, source_target_pairs={{0,6},{1,7},{2,4},{3,5},{4,2},{5,3},{6,0},{7,1},{8,14},{9,15},{10,... | collective-permute-start | bytes 24584 | tf_op jit(solution)/shard_map/ppermute | solution.py:381
  45.9 2.1 %collective-permute-done.11 = f32[16,128]{1,0:T(8,128)S(1)} collective-permute-done((f32[16,128]{1,0:T(8,128)S(1)}, f32[16,128]{1,0:T(8,128)S(1)}, u32[]{:S(2)}, u32[]{:S(2)}) %collective-permute-start.11) | collective-permute-done | bytes 8224 | tf_op jit(solution)/shard_map/ppermute | solution.py:381
  50.8 5.0 %collective-permute-done.12 = bf16[776,128]{1,0:T(8,128)(2,1)S(1)} collective-permute-done((bf16[776,128]{1,0:T(8,128)(2,1)S(1)}, bf16[776,128]{1,0:T(8,128)(2,1)S(1)}, u32[]{:S(2)}, u32[]{:S(2)}) %collective-permute-start.12) | collective-permute-done | bytes 198688 | tf_op jit(solution)/shard_map/ppermute | solution.py:48
  56.6 2.6 %collective-permute-done.13 = bf16[776,128]{1,0:T(8,128)(2,1)S(1)} collective-permute-done((bf16[776,128]{1,0:T(8,128)(2,1)S(1)}, bf16[776,128]{1,0:T(8,128)(2,1)S(1)}, u32[]{:S(2)}, u32[]{:S(2)}) %collective-permute-start.13) | collective-permute-done | bytes 198688 | tf_op jit(solution)/shard_map/ppermute | solution.py:48
  59.3 3.2 %collective-permute-start.19 = (bf16[2,776,128]{2,1,0:T(8,128)(2,1)S(1)}, bf16[2,776,128]{2,1,0:T(8,128)(2,1)S(1)}, u32[]{:S(2)}, u32[]{:S(2)}) collective-permute-start(bf16[2,776,128]{2,1,0:T(8,128)(2,1)S(1)} %pad_maximum_fusion.1.refs_1_), channel_id=1, source_target_pairs={{0,8},{1,33},{2,10},{3,35},{4,12},{5,37},{6,14},{7,39},{8,16},{9,4... | collective-permute-start | bytes 1191944 | tf_op jit(solution)/shard_map/ppermute | solution.py:48
  63.7 2.1 %collective-permute-start.16 = (bf16[2,776,128]{2,1,0:T(8,128)(2,1)S(1)}, bf16[2,776,128]{2,1,0:T(8,128)(2,1)S(1)}, u32[]{:S(2)}, u32[]{:S(2)}) collective-permute-start(bf16[2,776,128]{2,1,0:T(8,128)(2,1)S(1)} %collective-permute-done.15.refs_4_), channel_id=1, source_target_pairs={{0,8},{1,33},{2,10},{3,35},{4,12},{5,37},{6,14},{7,39},{8,16},{9,4... | collective-permute-start | bytes 1191944 | tf_op jit(solution)/shard_map/ppermute | solution.py:48
  65.8 2.6 %collective-permute-done.17.refs_7_ = bf16[2,776,128]{2,1,0:T(8,128)(2,1)S(1)} collective-permute-done((bf16[2,776,128]{2,1,0:T(8,128)(2,1)S(1)}, bf16[2,776,128]{2,1,0:T(8,128)(2,1)S(1)}, u32[]{:S(2)}, u32[]{:S(2)}) %collective-permute-start.17) | collective-permute-done | bytes 397344 | tf_op jit(solution)/shard_map/ppermute | solution.py:48
  69.5 3.1 %collective-permute-done.20.refs_6_ = bf16[2,776,128]{2,1,0:T(8,128)(2,1)S(1)} collective-permute-done((bf16[2,776,128]{2,1,0:T(8,128)(2,1)S(1)}, bf16[2,776,128]{2,1,0:T(8,128)(2,1)S(1)}, u32[]{:S(2)}, u32[]{:S(2)}) %collective-permute-start.20) | collective-permute-done | bytes 397344 | tf_op jit(solution)/shard_map/ppermute | solution.py:48
  72.6 4.8 %collective-permute-done.18.refs_3_ = bf16[2,776,128]{2,1,0:T(8,128)(2,1)S(1)} collective-permute-done((bf16[2,776,128]{2,1,0:T(8,128)(2,1)S(1)}, bf16[2,776,128]{2,1,0:T(8,128)(2,1)S(1)}, u32[]{:S(2)}, u32[]{:S(2)}) %collective-permute-start.18) | collective-permute-done | bytes 397344 | tf_op jit(solution)/shard_map/ppermute | solution.py:48
  77.4 2.9 %unpack.1 = (bf16[1024,512]{1,0:T(8,128)(2,1)}, bf16[1024,128]{1,0:T(8,128)(2,1)}, bf16[1024,128]{1,0:T(8,128)(2,1)}, bf16[1024,128]{1,0:T(8,128)(2,1)}, bf16[51...) custom-call(s32[3]{0:T(128)S(1)} %pad_add_fusion.at_ref, ...), custom_call_target="tpu_custom_call" | custom-call | tf_op jit(solution)/shard_map/unpack/pallas_call | solution.py:332
  (75 shorter events, 12.8 us)
Async XLA Ops:
  4.4 7.8 %collective-permute-start = (f16[768,256]{1,0:T(8,128)(2,1)S(1)}, f16[768,256]{1,0:T(8,128)(2,1)S(1)}, u32[]{:S(2)}, u32[]{:S(2)}) collective-permute-start(f16[768,256]{1,0:T(8,128)(2,1)S(1)} %bitcast.99), channel_id=1, source_target_pairs={{0,8},{1,33},{2,10},{3,35},{4,12},{5,37},{6,14},{7,39},{8,16},{9,4... | collective-permute-start | bytes 1179656 | tf_op jit(solution)/shard_map/ppermute | solution.py:48
  4.8 9.1 %collective-permute-start.1 = (f16[776,256]{1,0:T(8,128)(2,1)S(1)}, f16[776,256]{1,0:T(8,128)(2,1)S(1)}, u32[]{:S(2)}, u32[]{:S(2)}) collective-permute-start(f16[776,256]{1,0:T(8,128)(2,1)S(1)} %get-tuple-element.83), channel_id=1, source_target_pairs={{0,24},{1,97},{2,26},{3,99},{4,28},{5,101},{6,30},{7,103},{8,0},{9... | collective-permute-start | bytes 1191944 | tf_op jit(solution)/shard_map/ppermute | solution.py:48
  6.7 11.3 %collective-permute-start.2 = (f16[768,256]{1,0:T(8,128)(2,1)S(1)}, f16[768,256]{1,0:T(8,128)(2,1)S(1)}, u32[]{:S(2)}, u32[]{:S(2)}) collective-permute-start(f16[768,256]{1,0:T(8,128)(2,1)S(1)} %bitcast.98), channel_id=1, source_target_pairs={{0,24},{1,97},{2,26},{3,99},{4,28},{5,101},{6,30},{7,103},{8,0},{9... | collective-permute-start | bytes 1179656 | tf_op jit(solution)/shard_map/ppermute | solution.py:48
  7.5 13.4 %collective-permute-start.4 = (f16[776,256]{1,0:T(8,128)(2,1)S(1)}, f16[776,256]{1,0:T(8,128)(2,1)S(1)}, u32[]{:S(2)}, u32[]{:S(2)}) collective-permute-start(f16[776,256]{1,0:T(8,128)(2,1)S(1)} %get-tuple-element.82), channel_id=1, source_target_pairs={{0,8},{1,33},{2,10},{3,35},{4,12},{5,37},{6,14},{7,39},{8,16},{9,4... | collective-permute-start | bytes 1191944 | tf_op jit(solution)/shard_map/ppermute | solution.py:48
  12.4 8.3 %collective-permute-start.3 = (f16[768,256]{1,0:T(8,128)(2,1)S(1)}, f16[768,256]{1,0:T(8,128)(2,1)S(1)}, u32[]{:S(2)}, u32[]{:S(2)}) collective-permute-start(f16[768,256]{1,0:T(8,128)(2,1)S(1)} %fusion.7), channel_id=1, source_target_pairs={{0,8},{1,33},{2,10},{3,35},{4,12},{5,37},{6,14},{7,39},{8,16},{9,4... | collective-permute-start | bytes 1179656 | tf_op jit(solution)/shard_map/ppermute | solution.py:48
  14.0 9.1 %collective-permute-start.5 = (f16[776,256]{1,0:T(8,128)(2,1)S(1)}, f16[776,256]{1,0:T(8,128)(2,1)S(1)}, u32[]{:S(2)}, u32[]{:S(2)}) collective-permute-start(f16[776,256]{1,0:T(8,128)(2,1)S(1)} %fusion.3), channel_id=1, source_target_pairs={{0,24},{1,97},{2,26},{3,99},{4,28},{5,101},{6,30},{7,103},{8,0},{9... | collective-permute-start | bytes 1191944 | tf_op jit(solution)/shard_map/ppermute | solution.py:48
  24.2 23.8 %copy-start.2 = (f32[64,512]{1,0:T(8,128)S(1)}, f32[64,512]{1,0:T(8,128)}, u32[]{:S(2)}) copy-start(f32[64,512]{1,0:T(8,128)} %refs_8_.3) | copy-start | bytes 393220
  24.2 23.7 %copy-start.3 = (f32[512,64]{0,1:T(8,128)S(1)}, f32[512,64]{0,1:T(8,128)}, u32[]{:S(2)}) copy-start(f32[512,64]{0,1:T(8,128)} %param.41) | copy-start | bytes 393220
  24.2 23.7 %copy-start.8 = (f32[64,128]{1,0:T(8,128)S(1)}, f32[64,128]{1,0:T(8,128)}, u32[]{:S(2)}) copy-start(f32[64,128]{1,0:T(8,128)} %refs_9_.3) | copy-start | bytes 98308
  24.6 7.4 %collective-permute-start.8 = (f16[776,128]{1,0:T(8,128)(2,1)S(1)}, f16[776,128]{1,0:T(8,128)(2,1)S(1)}, u32[]{:S(2)}, u32[]{:S(2)}) collective-permute-start(f16[776,128]{1,0:T(8,128)(2,1)S(1)} %get-tuple-element.88), channel_id=1, source_target_pairs={{0,96},{1,25},{2,98},{3,27},{4,100},{5,29},{6,102},{7,31},{8,104},... | collective-permute-start | bytes 595976 | tf_op jit(solution)/shard_map/ppermute | solution.py:48
  28.8 9.0 %collective-permute-start.7 = (f16[776,128]{1,0:T(8,128)(2,1)S(1)}, f16[776,128]{1,0:T(8,128)(2,1)S(1)}, u32[]{:S(2)}, u32[]{:S(2)}) collective-permute-start(f16[776,128]{1,0:T(8,128)(2,1)S(1)} %get-tuple-element.89), channel_id=1, source_target_pairs={{0,32},{1,9},{2,34},{3,11},{4,36},{5,13},{6,38},{7,15},{8,40},{9,1... | collective-permute-start | bytes 595976 | tf_op jit(solution)/shard_map/ppermute | solution.py:48
  28.8 9.0 %collective-permute-start.6 = (f16[776,128]{1,0:T(8,128)(2,1)S(1)}, f16[776,128]{1,0:T(8,128)(2,1)S(1)}, u32[]{:S(2)}, u32[]{:S(2)}) collective-permute-start(f16[776,128]{1,0:T(8,128)(2,1)S(1)} %get-tuple-element.87), channel_id=1, source_target_pairs={{0,64},{1,17},{2,66},{3,19},{4,68},{5,21},{6,70},{7,23},{8,72},{9,... | collective-permute-start | bytes 595976 | tf_op jit(solution)/shard_map/ppermute | solution.py:48
  38.2 1.2 %collective-permute-start.9 = (f32[16,128]{1,0:T(8,128)S(1)}, f32[16,128]{1,0:T(8,128)S(1)}, u32[]{:S(2)}, u32[]{:S(2)}) collective-permute-start(f32[16,128]{1,0:T(8,128)S(1)} %norms.1), channel_id=1, source_target_pairs={{0,1},{1,0},{2,3},{3,2},{4,5},{5,4},{6,7},{7,6},{8,9},{9,8},{10,11... | collective-permute-start | bytes 24584 | tf_op jit(solution)/shard_map/ppermute | solution.py:381
  39.5 3.7 %collective-permute-start.10 = (f32[16,128]{1,0:T(8,128)S(1)}, f32[16,128]{1,0:T(8,128)S(1)}, u32[]{:S(2)}, u32[]{:S(2)}) collective-permute-start(f32[16,128]{1,0:T(8,128)S(1)} %add.45), channel_id=1, source_target_pairs={{0,2},{1,3},{2,0},{3,1},{4,6},{5,7},{6,4},{7,5},{8,10},{9,11},{10,... | collective-permute-start | bytes 24584 | tf_op jit(solution)/shard_map/ppermute | solution.py:381
  43.1 4.9 %collective-permute-start.11 = (f32[16,128]{1,0:T(8,128)S(1)}, f32[16,128]{1,0:T(8,128)S(1)}, u32[]{:S(2)}, u32[]{:S(2)}) collective-permute-start(f32[16,128]{1,0:T(8,128)S(1)} %add.46), channel_id=1, source_target_pairs={{0,6},{1,7},{2,4},{3,5},{4,2},{5,3},{6,0},{7,1},{8,14},{9,15},{10,... | collective-permute-start | bytes 24584 | tf_op jit(solution)/shard_map/ppermute | solution.py:381
  48.4 7.4 %collective-permute-start.12 = (bf16[776,128]{1,0:T(8,128)(2,1)S(1)}, bf16[776,128]{1,0:T(8,128)(2,1)S(1)}, u32[]{:S(2)}, u32[]{:S(2)}) collective-permute-start(bf16[776,128]{1,0:T(8,128)(2,1)S(1)} %halves.1), channel_id=1, source_target_pairs={{0,64},{1,17},{2,66},{3,19},{4,68},{5,21},{6,70},{7,23},{8,72},{9,... | collective-permute-start | bytes 595976 | tf_op jit(solution)/shard_map/ppermute | solution.py:48
  48.8 7.8 %collective-permute-start.14 = (bf16[776,128]{1,0:T(8,128)(2,1)S(1)}, bf16[776,128]{1,0:T(8,128)(2,1)S(1)}, u32[]{:S(2)}, u32[]{:S(2)}) collective-permute-start(bf16[776,128]{1,0:T(8,128)(2,1)S(1)} %halves.1), channel_id=1, source_target_pairs={{0,96},{1,25},{2,98},{3,27},{4,100},{5,29},{6,102},{7,31},{8,104},... | collective-permute-start | bytes 595976 | tf_op jit(solution)/shard_map/ppermute | solution.py:48
  49.9 9.2 %collective-permute-start.13 = (bf16[776,128]{1,0:T(8,128)(2,1)S(1)}, bf16[776,128]{1,0:T(8,128)(2,1)S(1)}, u32[]{:S(2)}, u32[]{:S(2)}) collective-permute-start(bf16[776,128]{1,0:T(8,128)(2,1)S(1)} %halves.1), channel_id=1, source_target_pairs={{0,32},{1,9},{2,34},{3,11},{4,36},{5,13},{6,38},{7,15},{8,40},{9,1... | collective-permute-start | bytes 595976 | tf_op jit(solution)/shard_map/ppermute | solution.py:48
  55.8 7.9 %collective-permute-start.15 = (bf16[2,776,128]{2,1,0:T(8,128)(2,1)S(1)}, bf16[2,776,128]{2,1,0:T(8,128)(2,1)S(1)}, u32[]{:S(2)}, u32[]{:S(2)}) collective-permute-start(bf16[2,776,128]{2,1,0:T(8,128)(2,1)S(1)} %pad_maximum_fusion.refs_0_), channel_id=1, source_target_pairs={{0,8},{1,33},{2,10},{3,35},{4,12},{5,37},{6,14},{7,39},{8,16},{9,4... | collective-permute-start | bytes 1191944 | tf_op jit(solution)/shard_map/ppermute | solution.py:48
  59.2 9.1 %collective-permute-start.17 = (bf16[2,776,128]{2,1,0:T(8,128)(2,1)S(1)}, bf16[2,776,128]{2,1,0:T(8,128)(2,1)S(1)}, u32[]{:S(2)}, u32[]{:S(2)}) collective-permute-start(bf16[2,776,128]{2,1,0:T(8,128)(2,1)S(1)} %pad_maximum_fusion.1.refs_1_), channel_id=1, source_target_pairs={{0,24},{1,97},{2,26},{3,99},{4,28},{5,101},{6,30},{7,103},{8,0},{9... | collective-permute-start | bytes 1191944 | tf_op jit(solution)/shard_map/ppermute | solution.py:48
  59.3 10.2 %collective-permute-start.19 = (bf16[2,776,128]{2,1,0:T(8,128)(2,1)S(1)}, bf16[2,776,128]{2,1,0:T(8,128)(2,1)S(1)}, u32[]{:S(2)}, u32[]{:S(2)}) collective-permute-start(bf16[2,776,128]{2,1,0:T(8,128)(2,1)S(1)} %pad_maximum_fusion.1.refs_1_), channel_id=1, source_target_pairs={{0,8},{1,33},{2,10},{3,35},{4,12},{5,37},{6,14},{7,39},{8,16},{9,4... | collective-permute-start | bytes 1191944 | tf_op jit(solution)/shard_map/ppermute | solution.py:48
  62.5 10.1 %collective-permute-start.20 = (bf16[2,776,128]{2,1,0:T(8,128)(2,1)S(1)}, bf16[2,776,128]{2,1,0:T(8,128)(2,1)S(1)}, u32[]{:S(2)}, u32[]{:S(2)}) collective-permute-start(bf16[2,776,128]{2,1,0:T(8,128)(2,1)S(1)} %pad_maximum_fusion.refs_0_), channel_id=1, source_target_pairs={{0,24},{1,97},{2,26},{3,99},{4,28},{5,101},{6,30},{7,103},{8,0},{9... | collective-permute-start | bytes 1191944 | tf_op jit(solution)/shard_map/ppermute | solution.py:48
  63.7 8.9 %collective-permute-start.16 = (bf16[2,776,128]{2,1,0:T(8,128)(2,1)S(1)}, bf16[2,776,128]{2,1,0:T(8,128)(2,1)S(1)}, u32[]{:S(2)}, u32[]{:S(2)}) collective-permute-start(bf16[2,776,128]{2,1,0:T(8,128)(2,1)S(1)} %collective-permute-done.15.refs_4_), channel_id=1, source_target_pairs={{0,8},{1,33},{2,10},{3,35},{4,12},{5,37},{6,14},{7,39},{8,16},{9,4... | collective-permute-start | bytes 1191944 | tf_op jit(solution)/shard_map/ppermute | solution.py:48
  68.3 9.0 %collective-permute-start.18 = (bf16[2,776,128]{2,1,0:T(8,128)(2,1)S(1)}, bf16[2,776,128]{2,1,0:T(8,128)(2,1)S(1)}, u32[]{:S(2)}, u32[]{:S(2)}) collective-permute-start(bf16[2,776,128]{2,1,0:T(8,128)(2,1)S(1)} %collective-permute-done.17.refs_7_), channel_id=1, source_target_pairs={{0,24},{1,97},{2,26},{3,99},{4,28},{5,101},{6,30},{7,103},{8,0},{9... | collective-permute-start | bytes 1191944 | tf_op jit(solution)/shard_map/ppermute | solution.py:48
  (13 other events, 248.9 us)

commit v2 on v1

--- a/solution.py
+++ b/solution.py
@@ -288,60 +288,110 @@
     return out[:8], out[8:]
 
 
-def unpack_kernel(at_ref, *refs):
-    stacks, (up, query, key, value, down, mixed, vectors, *scratch) = refs[:8], refs[8:]
-    up_s, query_s, key_s, value_s, down_s, mixed_s, rest_s, sems = scratch
-    for n, d in enumerate(ORDER):
+def early_kernel(at_ref, *refs):
+    stacks = {0: refs[0:2], 1: refs[2:4], 3: refs[4:6]}
+    up, query, key, value, down_s, mixed_s, vectors, up_s, query_s, key_s, value_s, rest_s, sems = refs[6:]
+    for d in range(4):
         for k, e in enumerate(ORDER):
-            s, i = stacks[2 * n + k // 2], k % 2
             r = block_of(at_ref, (at_ref[0] - d) & 3, (at_ref[1] - e) & 3)
             rows = pl.ds(pl.multiple_of(r * B, B), B)
+            block = stacks[d][k // 2][k % 2] if d != 2 else jnp.zeros((T, 128), jnp.bfloat16)
             for c in range(4):
-                up_s[rows, c * 128 : c * 128 + 128] = s[i, c * B : c * B + B, :]
-            query_s[rows, :] = s[i, 4 * B : 5 * B, :]
-            key_s[rows, :] = s[i, 5 * B : 6 * B, :]
-            value_s[rows, :] = s[i, 6 * B : 7 * B, :]
-            rest_s[pl.ds(r, 1)] = s[i, 7 * B :, :][None]
-    pairs = ((up_s, up), (query_s, query), (key_s, key), (value_s, value), (down_s, down), (mixed_s, mixed))
-    copies = [pltpu.make_async_copy(a, b, sems.at[k]) for k, (a, b) in enumerate(pairs)]
-    for k in range(4):
-        copies[k].start()
+                up_s[rows, c * 128 : c * 128 + 128] = block[c * B : c * B + B, :]
+            query_s[rows, :] = block[4 * B : 5 * B, :]
+            key_s[rows, :] = block[5 * B : 6 * B, :]
+            value_s[rows, :] = block[6 * B : 7 * B, :]
+            rest_s[pl.ds(r, 1)] = block[7 * B :, :][None]
+    pairs = ((up_s, up), (query_s, query), (key_s, key), (value_s, value))
+    copies = [pltpu.make_async_copy(x, y, sems.at[k]) for k, (x, y) in enumerate(pairs)]
+    for one in copies:
+        one.start()
     lane = lax.broadcasted_iota(jnp.int32, (8, 128), 1)
     for p in range(8):
         lanes = slice(p * 128, p * 128 + 128)
         for k in range(5):
-            one = [rest_s[2 * p + j, k * B : k * B + B, :] for j in range(2)]
-            tile = jnp.concatenate(one, axis=0).T
+            tile = jnp.concatenate([rest_s[2 * p + j, k * B : k * B + B, :] for j in range(2)], axis=0).T
             if k < 4:
                 down_s[k * 128 : k * 128 + 128, lanes] = tile
             else:
                 mixed_s[:, lanes] = tile
-        one = [rest_s[2 * p + j, 5 * B :, :].astype(jnp.float32) for j in range(2)]
-        last = jnp.where(lane < B, one[0], one[1])
+        both = [rest_s[2 * p + j, 5 * B :, :].astype(jnp.float32) for j in range(2)]
+        last = jnp.where(lane < B, both[0], both[1])
         vectors[p : p + 1, :] = last[0:1]
         vectors[8 + p : 9 + p, :] = last[1:2]
-    for k in range(4, 6):
-        copies[k].start()
-    for c in copies:
-        c.wait()
-
-
-def unpack(place, stacks):
+    for one in copies:
+        one.wait()
+
+
+def late_kernel(at_ref, a, b, *refs):
+    up, query, key, value, down_s, mixed_s, vectors, down, mixed, up_s, thin_s, sems = refs[7:]
+    copies = []
+
+    def copy(source, target):
+        copies.append(pltpu.make_async_copy(source, target, sems.at[len(copies)]))
+        copies[-1].start()
+
+    half = lax.broadcasted_iota(jnp.int32, (128, 128), 1) >> 6
+    for i, e in enumerate(ORDER):
+        block = (a, b)[i // 2].at[i % 2]
+        r = block_of(at_ref, (at_ref[0] - 2) & 3, (at_ref[1] - e) & 3)
+        rows = pl.ds(pl.multiple_of(r * B, B), B)
+        for c in range(4):
+            up_s[i, :, c * 128 : c * 128 + 128] = block[c * B : c * B + B, :]
+        copy(up_s.at[i], up.at[rows])
+        for c, target in enumerate((query, key, value)):
+            thin_s[i, c] = block[(4 + c) * B : (5 + c) * B, :]
+            copy(thin_s.at[i, c], target.at[rows])
+        lanes = pl.ds(pl.multiple_of((r >> 1) * 128, 128), 128)
+        mine = half == (r & 1)
+        for k in range(5):
+            one = block[(7 + k) * B : (8 + k) * B, :]
+            tile = jnp.concatenate([one, one], axis=0).T.astype(jnp.float32)
+            ref, to = (down_s, slice(k * 128, k * 128 + 128)) if k < 4 else (mixed_s, slice(None))
+            ref[to, lanes] = jnp.where(mine, tile, ref[to, lanes].astype(jnp.float32)).astype(jnp.bfloat16)
+        last = block[12 * B :, :].astype(jnp.float32)
+        for k in range(2):
+            to = pl.ds(k * 8 + (r >> 1), 1)
+            vectors[to, :] = jnp.where(mine[0:1], last[k : k + 1], vectors[to, :])
+    copy(down_s, down)
+    copy(mixed_s, mixed)
+    for one in copies:
+        one.wait()
+
+
+def unpack(place, early, late):
     bf16 = jnp.bfloat16
     shapes = ((1024, 512), (1024, 128), (1024, 128), (1024, 128), (512, 1024), (128, 1024))
-    return pl.pallas_call(
-        unpack_kernel,
-        in_specs=[SM] + [VM] * 8,
-        out_specs=(*[HB] * 6, VM),
-        out_shape=(*[jax.ShapeDtypeStruct(s, bf16) for s in shapes], pltpu.VMEM((16, 128), jnp.float32)),
+    outs = [jax.ShapeDtypeStruct(s, bf16) for s in shapes]
+    kept = [pltpu.VMEM(s, bf16) for s in shapes[4:]] + [pltpu.VMEM((16, 128), jnp.float32)]
+    first = pl.pallas_call(
+        early_kernel,
+        in_specs=[SM] + [VM] * 6,
+        out_specs=(*[HB] * 4, *[VM] * 3),
+        out_shape=(*outs[:4], *kept),
         scratch_shapes=[
-            *[pltpu.VMEM(s, bf16) for s in shapes],
+            *[pltpu.VMEM(s, bf16) for s in shapes[:4]],
             pltpu.VMEM((16, 5 * B + 8, 128), bf16),
-            pltpu.SemaphoreType.DMA((6,)),
+            pltpu.SemaphoreType.DMA((4,)),
         ],
         compiler_params=PARAMS,
-        name="unpack",
-    )(place, *[vmem(s) for s in stacks])
+        name="unpack_early",
+    )(place, *[vmem(x) for x in early])
+    up, query, key, value, _, _, vectors, down, mixed = pl.pallas_call(
+        late_kernel,
+        in_specs=[SM, VM, VM] + [HB] * 4 + [VM] * 3,
+        out_specs=(*[HB] * 4, *[VM] * 3, HB, HB),
+        out_shape=(*outs[:4], *kept, *outs[4:]),
+        input_output_aliases={3 + k: k for k in range(7)},
+        scratch_shapes=[
+            pltpu.VMEM((4, B, 512), bf16),
+            pltpu.VMEM((4, 3, B, 128), bf16),
+            pltpu.SemaphoreType.DMA((18,)),
+        ],
+        compiler_params=PARAMS,
+        name="unpack_late",
+    )(place, *[vmem(x) for x in late], *[hbm(x) for x in first[:4]], *[vmem(x) for x in first[4:]])
+    return up, query, key, value, down, mixed, vectors
 
 
 def local(*args):
@@ -386,9 +436,8 @@
     one_a, three_a = marked(own_a, 1, 0), marked(own_a, 3, 0)
     three_b, one_b = marked(own_b, 3, 0), marked(own_b, 1, 0)
     two_a, two_b = send(one_a, 0, 1), send(three_b, 0, 3)
-    stacks = [own_a, own_b, two_a, two_b, one_a, one_b, three_a, three_b]
     nexts, news = update(lax.optimization_barrier((parts, own_a, own_b))[0], total, params, states)
-    up, query, key, value, down, mixed, vectors = unpack(place, stacks)
+    up, query, key, value, down, mixed, vectors = unpack(place, (own_a, own_b, one_a, one_b, three_a, three_b), (two_a, two_b))
     vectors = vectors.astype(bf16)
     norm, bias = vectors[:8].reshape(1024), vectors[8:].reshape(1024)
 

time: 81 us -> 79.6 us (0.983)
  waiting for transfers between devices: 40 us -> 35.6 us
  Pallas kernels: 11.5 us -> 13.1 us
  starting transfers between devices: 26 us -> 27.3 us
    ppermute x18, waiting for transfers between devices: 34.5 us -> 30.2 us  [send(): return lax.ppermute(x, ('replica', 'model'), pairs)]
    pallas_call x1 -> x2, Pallas kernels: 2.92 us -> 4.56 us  [the longest x1 2.46 us: unpack(): pl.pallas_call(early_kernel, in_specs=[SM] + [VM] * 6, out_specs=(*[HB] *...]
    ppermute x18, starting transfers between devices: 21.7 us -> 23 us  [send(): return lax.ppermute(x, ('replica', 'model'), pairs)]
  transfers between devices with their start and end apart: 21 -> 21, of which waited for: 17 -> 18; matrix products, arithmetic and copies ran while one was open for 1% -> 1% of each run, Pallas kernels for 5% -> 8%
where the time goes in v2:
time: 79.6 us; the launch traced here: 79.4 us
  waiting for transfers between devices  35.6 us (45%)
  starting transfers between devices  27.3 us (34%)
  Pallas kernels  13.1 us (16%)
  other arithmetic  1.59 us (2%)
  between operations  1.07 us (1%)
  local copies, waits for them, and re-layouts  0.81 us (1%)
    ppermute x18, waiting for transfers between devices, send(): return lax.ppermute(x, ('replica', 'model'), pairs)  30.2 us
    ppermute x18, starting transfers between devices, send(): return lax.ppermute(x, ('replica', 'model'), pairs)  23 us
    pallas_call x2, Pallas kernels, pack(): pl.pallas_call(kernel, in_specs=[SM] + [HB] * 8, out_specs=(VM, VM), out_...  6.04 us
    ppermute x3, waiting for transfers between devices, local(): lax.ppermute(parts, 'model', [(m, partner(m)) for m in range(8)])  5.42 us
    ppermute x3, starting transfers between devices, local(): lax.ppermute(parts, 'model', [(m, partner(m)) for m in range(8)])  4.29 us
    pallas_call x1, Pallas kernels, unpack(): pl.pallas_call(early_kernel, in_specs=[SM] + [VM] * 6, out_specs=(*[HB] *...  2.46 us
    pallas_call x1, Pallas kernels, unpack(): pl.pallas_call(late_kernel, in_specs=[SM, VM, VM] + [HB] * 4 + [VM] * 3,...  2.1 us
  transfers between devices with their start and end apart: 21, of which 18 were waited for; matrix products, arithmetic and copies ran while one was open for 1% of the time, Pallas kernels for 8%

profile of v2, /device:TPU:24, one launch (start us, length us, event | category | flops | bytes accessed | tf_op | source)
XLA Modules:
  0.0 79.4 jit_solution(7879420942739212436)
XLA Ops:
  0.7 3.4 %shard_map.415 = (f32[3,4,192,256]{3,2,1,0:T(8,128)S(1)}, f32[3,776,256]{2,1,0:T(8,128)S(1)}) custom-call(s32[3]{0:T(128)S(1)} %pad_add_fusion.at_ref, f32[4,4,64,512]{3,2,1,0:T(8,128)} %bitcast.90, f32[4,4,64,128]{3,2,1,0:T(8,128)} %bitcast.92, f32[4,4,64,128]{3,2,1,0:T(8,128)} %bitcast.94, f32[1024,128]{1,0:T(8,128)} %bitcast.96, f32[1,512,1024]{2,1,0:T(8,128)} %down.3, ...), custom_call_target="tpu_custom_call" | custom-call | tf_op jit(solution)/shard_map/pallas_call | solution.py:141
  4.8 2.0 %collective-permute-start.1 = (f16[776,256]{1,0:T(8,128)(2,1)S(1)}, f16[776,256]{1,0:T(8,128)(2,1)S(1)}, u32[]{:S(2)}, u32[]{:S(2)}) collective-permute-start(f16[776,256]{1,0:T(8,128)(2,1)S(1)} %get-tuple-element.97), channel_id=1, source_target_pairs={{0,24},{1,97},{2,26},{3,99},{4,28},{5,101},{6,30},{7,103},{8,0},{9... | collective-permute-start | bytes 1191944 | tf_op jit(solution)/shard_map/ppermute | solution.py:48
  7.5 2.5 %collective-permute-start.4 = (f16[776,256]{1,0:T(8,128)(2,1)S(1)}, f16[776,256]{1,0:T(8,128)(2,1)S(1)}, u32[]{:S(2)}, u32[]{:S(2)}) collective-permute-start(f16[776,256]{1,0:T(8,128)(2,1)S(1)} %get-tuple-element.96), channel_id=1, source_target_pairs={{0,8},{1,33},{2,10},{3,35},{4,12},{5,37},{6,14},{7,39},{8,16},{9,4... | collective-permute-start | bytes 1191944 | tf_op jit(solution)/shard_map/ppermute | solution.py:48
  10.0 2.3 %collective-permute-done = f16[768,256]{1,0:T(8,128)(2,1)S(1)} collective-permute-done((f16[768,256]{1,0:T(8,128)(2,1)S(1)}, f16[768,256]{1,0:T(8,128)(2,1)S(1)}, u32[]{:S(2)}, u32[]{:S(2)}) %collective-permute-start) | collective-permute-done | bytes 393248 | tf_op jit(solution)/shard_map/ppermute | solution.py:48
  14.8 2.7 %shard_map.416 = (f32[1,4,192,256]{3,2,1,0:T(8,128)S(1)}, f32[1,776,256]{2,1,0:T(8,128)S(1)}) custom-call(s32[3]{0:T(128)S(1)} %pad_add_fusion.at_ref, f32[4,4,64,512]{3,2,1,0:T(8,128)} %bitcast.91, f32[4,4,64,128]{3,2,1,0:T(8,128)} %bitcast.93, f32[4,4,64,128]{3,2,1,0:T(8,128)} %bitcast.95, f32[1024,128]{1,0:T(8,128)} %bitcast.97, f32[1,512,1024]{2,1,0:T(8,128)} %down.3, ...), custom_call_target="tpu_custom_call" | custom-call | tf_op jit(solution)/shard_map/pallas_call | solution.py:141
  18.1 2.6 %collective-permute-done.3 = f16[768,256]{1,0:T(8,128)(2,1)S(1)} collective-permute-done((f16[768,256]{1,0:T(8,128)(2,1)S(1)}, f16[768,256]{1,0:T(8,128)(2,1)S(1)}, u32[]{:S(2)}, u32[]{:S(2)}) %collective-permute-start.3) | collective-permute-done | bytes 393248 | tf_op jit(solution)/shard_map/ppermute | solution.py:48
  20.9 2.2 %collective-permute-done.5 = f16[776,256]{1,0:T(8,128)(2,1)S(1)} collective-permute-done((f16[776,256]{1,0:T(8,128)(2,1)S(1)}, f16[776,256]{1,0:T(8,128)(2,1)S(1)}, u32[]{:S(2)}, u32[]{:S(2)}) %collective-permute-start.5) | collective-permute-done | bytes 397344 | tf_op jit(solution)/shard_map/ppermute | solution.py:48
  24.6 4.1 %collective-permute-start.6 = (f16[776,128]{1,0:T(8,128)(2,1)S(1)}, f16[776,128]{1,0:T(8,128)(2,1)S(1)}, u32[]{:S(2)}, u32[]{:S(2)}) collective-permute-start(f16[776,128]{1,0:T(8,128)(2,1)S(1)} %get-tuple-element.101), channel_id=1, source_target_pairs={{0,64},{1,17},{2,66},{3,19},{4,68},{5,21},{6,70},{7,23},{8,72},{9,... | collective-permute-start | bytes 595976 | tf_op jit(solution)/shard_map/ppermute | solution.py:48
  30.7 1.6 %collective-permute-done.6 = f16[776,128]{1,0:T(8,128)(2,1)S(1)} collective-permute-done((f16[776,128]{1,0:T(8,128)(2,1)S(1)}, f16[776,128]{1,0:T(8,128)(2,1)S(1)}, u32[]{:S(2)}, u32[]{:S(2)}) %collective-permute-start.6) | collective-permute-done | bytes 198688 | tf_op jit(solution)/shard_map/ppermute | solution.py:48
  32.4 3.2 %collective-permute-done.8 = f16[776,128]{1,0:T(8,128)(2,1)S(1)} collective-permute-done((f16[776,128]{1,0:T(8,128)(2,1)S(1)}, f16[776,128]{1,0:T(8,128)(2,1)S(1)}, u32[]{:S(2)}, u32[]{:S(2)}) %collective-permute-start.8) | collective-permute-done | bytes 198688 | tf_op jit(solution)/shard_map/ppermute | solution.py:48
  37.9 1.5 %collective-permute-start.10 = (f32[16,128]{1,0:T(8,128)S(1)}, f32[16,128]{1,0:T(8,128)S(1)}, u32[]{:S(2)}, u32[]{:S(2)}) collective-permute-start(f32[16,128]{1,0:T(8,128)S(1)} %add.45), channel_id=1, source_target_pairs={{0,2},{1,3},{2,0},{3,1},{4,6},{5,7},{6,4},{7,5},{8,10},{9,11},{10,... | collective-permute-start | bytes 24584 | tf_op jit(solution)/shard_map/ppermute | solution.py:431
  39.4 2.2 %collective-permute-done.10 = f32[16,128]{1,0:T(8,128)S(1)} collective-permute-done((f32[16,128]{1,0:T(8,128)S(1)}, f32[16,128]{1,0:T(8,128)S(1)}, u32[]{:S(2)}, u32[]{:S(2)}) %collective-permute-start.10) | collective-permute-done | bytes 8224 | tf_op jit(solution)/shard_map/ppermute | solution.py:431
  41.6 2.8 %collective-permute-start.11 = (f32[16,128]{1,0:T(8,128)S(1)}, f32[16,128]{1,0:T(8,128)S(1)}, u32[]{:S(2)}, u32[]{:S(2)}) collective-permute-start(f32[16,128]{1,0:T(8,128)S(1)} %add.46), channel_id=1, source_target_pairs={{0,6},{1,7},{2,4},{3,5},{4,2},{5,3},{6,0},{7,1},{8,14},{9,15},{10,... | collective-permute-start | bytes 24584 | tf_op jit(solution)/shard_map/ppermute | solution.py:431
  44.4 2.1 %collective-permute-done.11 = f32[16,128]{1,0:T(8,128)S(1)} collective-permute-done((f32[16,128]{1,0:T(8,128)S(1)}, f32[16,128]{1,0:T(8,128)S(1)}, u32[]{:S(2)}, u32[]{:S(2)}) %collective-permute-start.11) | collective-permute-done | bytes 8224 | tf_op jit(solution)/shard_map/ppermute | solution.py:431
  46.9 1.8 %collective-permute-start.12 = (bf16[776,128]{1,0:T(8,128)(2,1)S(1)}, bf16[776,128]{1,0:T(8,128)(2,1)S(1)}, u32[]{:S(2)}, u32[]{:S(2)}) collective-permute-start(bf16[776,128]{1,0:T(8,128)(2,1)S(1)} %halves.1), channel_id=1, source_target_pairs={{0,64},{1,17},{2,66},{3,19},{4,68},{5,21},{6,70},{7,23},{8,72},{9,... | collective-permute-start | bytes 595976 | tf_op jit(solution)/shard_map/ppermute | solution.py:48
  50.7 3.5 %collective-permute-done.12 = bf16[776,128]{1,0:T(8,128)(2,1)S(1)} collective-permute-done((bf16[776,128]{1,0:T(8,128)(2,1)S(1)}, bf16[776,128]{1,0:T(8,128)(2,1)S(1)}, u32[]{:S(2)}, u32[]{:S(2)}) %collective-permute-start.12) | collective-permute-done | bytes 198688 | tf_op jit(solution)/shard_map/ppermute | solution.py:48
  55.5 3.1 %collective-permute-done.15 = bf16[776,128]{1,0:T(8,128)(2,1)S(1)} collective-permute-done((bf16[776,128]{1,0:T(8,128)(2,1)S(1)}, bf16[776,128]{1,0:T(8,128)(2,1)S(1)}, u32[]{:S(2)}, u32[]{:S(2)}) %collective-permute-start.15) | collective-permute-done | bytes 198688 | tf_op jit(solution)/shard_map/ppermute | solution.py:48
  59.2 2.8 %collective-permute-start.19 = (bf16[2,776,128]{2,1,0:T(8,128)(2,1)S(1)}, bf16[2,776,128]{2,1,0:T(8,128)(2,1)S(1)}, u32[]{:S(2)}, u32[]{:S(2)}) collective-permute-start(bf16[2,776,128]{2,1,0:T(8,128)(2,1)S(1)} %pad_maximum_fusion.1.refs_1_), channel_id=1, source_target_pairs={{0,8},{1,33},{2,10},{3,35},{4,12},{5,37},{6,14},{7,39},{8,16},{9,4... | collective-permute-start | bytes 1191944 | tf_op jit(solution)/shard_map/ppermute | solution.py:48
  62.1 1.9 %collective-permute-start.14 = (bf16[2,776,128]{2,1,0:T(8,128)(2,1)S(1)}, bf16[2,776,128]{2,1,0:T(8,128)(2,1)S(1)}, u32[]{:S(2)}, u32[]{:S(2)}) collective-permute-start(bf16[2,776,128]{2,1,0:T(8,128)(2,1)S(1)} %collective-permute-done.13.refs_2_), channel_id=1, source_target_pairs={{0,8},{1,33},{2,10},{3,35},{4,12},{5,37},{6,14},{7,39},{8,16},{9,4... | collective-permute-start | bytes 1191944 | tf_op jit(solution)/shard_map/ppermute | solution.py:48
  64.0 3.8 %collective-permute-done.17.refs_5_ = bf16[2,776,128]{2,1,0:T(8,128)(2,1)S(1)} collective-permute-done((bf16[2,776,128]{2,1,0:T(8,128)(2,1)S(1)}, bf16[2,776,128]{2,1,0:T(8,128)(2,1)S(1)}, u32[]{:S(2)}, u32[]{:S(2)}) %collective-permute-start.17) | collective-permute-done | bytes 397344 | tf_op jit(solution)/shard_map/ppermute | solution.py:48
  68.9 3.1 %collective-permute-done.20.refs_4_ = bf16[2,776,128]{2,1,0:T(8,128)(2,1)S(1)} collective-permute-done((bf16[2,776,128]{2,1,0:T(8,128)(2,1)S(1)}, bf16[2,776,128]{2,1,0:T(8,128)(2,1)S(1)}, u32[]{:S(2)}, u32[]{:S(2)}) %collective-permute-start.20) | collective-permute-done | bytes 397344 | tf_op jit(solution)/shard_map/ppermute | solution.py:48
  72.0 2.5 %unpack_early.1 = (bf16[1024,512]{1,0:T(8,128)(2,1)}, bf16[1024,128]{1,0:T(8,128)(2,1)}, bf16[1024,128]{1,0:T(8,128)(2,1)}, bf16[1024,128]{1,0:T(8,128)(2,1)}, b...) custom-call(s32[3]{0:T(128)S(1)} %pad_add_fusion.at_ref, ...), custom_call_target="tpu_custom_call" | custom-call | tf_op jit(solution)/shard_map/unpack_early/pallas_call | solution.py:367
  74.5 2.3 %collective-permute-done.18.b = bf16[2,776,128]{2,1,0:T(8,128)(2,1)S(1)} collective-permute-done((bf16[2,776,128]{2,1,0:T(8,128)(2,1)S(1)}, bf16[2,776,128]{2,1,0:T(8,128)(2,1)S(1)}, u32[]{:S(2)}, u32[]{:S(2)}) %collective-permute-start.18) | collective-permute-done | bytes 397344 | tf_op jit(solution)/shard_map/ppermute | solution.py:48
  76.7 2.1 %unpack_late.1 = (bf16[1024,512]{1,0:T(8,128)(2,1)}, bf16[1024,128]{1,0:T(8,128)(2,1)}, bf16[1024,128]{1,0:T(8,128)(2,1)}, bf16[1024,128]{1,0:T(8,128)(2,1)}, bf...) custom-call(s32[3]{0:T(128)S(1)} %pad_add_fusion.at_ref, ...), custom_call_target="tpu_custom_call", output_to_operand_aliasing={{0}: (3, {}), {1}: (4, {}), {2}: (5, {}), {3}: (6, {}), {4}... | custom-call | tf_op jit(solution)/shard_map/unpack_late/pallas_call | solution.py:380
  (76 shorter events, 16.6 us)
Async XLA Ops:
  4.4 7.8 %collective-permute-start = (f16[768,256]{1,0:T(8,128)(2,1)S(1)}, f16[768,256]{1,0:T(8,128)(2,1)S(1)}, u32[]{:S(2)}, u32[]{:S(2)}) collective-permute-start(f16[768,256]{1,0:T(8,128)(2,1)S(1)} %bitcast.99), channel_id=1, source_target_pairs={{0,8},{1,33},{2,10},{3,35},{4,12},{5,37},{6,14},{7,39},{8,16},{9,4... | collective-permute-start | bytes 1179656 | tf_op jit(solution)/shard_map/ppermute | solution.py:48
  4.8 9.1 %collective-permute-start.1 = (f16[776,256]{1,0:T(8,128)(2,1)S(1)}, f16[776,256]{1,0:T(8,128)(2,1)S(1)}, u32[]{:S(2)}, u32[]{:S(2)}) collective-permute-start(f16[776,256]{1,0:T(8,128)(2,1)S(1)} %get-tuple-element.97), channel_id=1, source_target_pairs={{0,24},{1,97},{2,26},{3,99},{4,28},{5,101},{6,30},{7,103},{8,0},{9... | collective-permute-start | bytes 1191944 | tf_op jit(solution)/shard_map/ppermute | solution.py:48
  6.7 11.3 %collective-permute-start.2 = (f16[768,256]{1,0:T(8,128)(2,1)S(1)}, f16[768,256]{1,0:T(8,128)(2,1)S(1)}, u32[]{:S(2)}, u32[]{:S(2)}) collective-permute-start(f16[768,256]{1,0:T(8,128)(2,1)S(1)} %bitcast.98), channel_id=1, source_target_pairs={{0,24},{1,97},{2,26},{3,99},{4,28},{5,101},{6,30},{7,103},{8,0},{9... | collective-permute-start | bytes 1179656 | tf_op jit(solution)/shard_map/ppermute | solution.py:48
  7.5 13.4 %collective-permute-start.4 = (f16[776,256]{1,0:T(8,128)(2,1)S(1)}, f16[776,256]{1,0:T(8,128)(2,1)S(1)}, u32[]{:S(2)}, u32[]{:S(2)}) collective-permute-start(f16[776,256]{1,0:T(8,128)(2,1)S(1)} %get-tuple-element.96), channel_id=1, source_target_pairs={{0,8},{1,33},{2,10},{3,35},{4,12},{5,37},{6,14},{7,39},{8,16},{9,4... | collective-permute-start | bytes 1191944 | tf_op jit(solution)/shard_map/ppermute | solution.py:48
  12.4 8.3 %collective-permute-start.3 = (f16[768,256]{1,0:T(8,128)(2,1)S(1)}, f16[768,256]{1,0:T(8,128)(2,1)S(1)}, u32[]{:S(2)}, u32[]{:S(2)}) collective-permute-start(f16[768,256]{1,0:T(8,128)(2,1)S(1)} %fusion.7), channel_id=1, source_target_pairs={{0,8},{1,33},{2,10},{3,35},{4,12},{5,37},{6,14},{7,39},{8,16},{9,4... | collective-permute-start | bytes 1179656 | tf_op jit(solution)/shard_map/ppermute | solution.py:48
  14.0 9.1 %collective-permute-start.5 = (f16[776,256]{1,0:T(8,128)(2,1)S(1)}, f16[776,256]{1,0:T(8,128)(2,1)S(1)}, u32[]{:S(2)}, u32[]{:S(2)}) collective-permute-start(f16[776,256]{1,0:T(8,128)(2,1)S(1)} %fusion.3), channel_id=1, source_target_pairs={{0,24},{1,97},{2,26},{3,99},{4,28},{5,101},{6,30},{7,103},{8,0},{9... | collective-permute-start | bytes 1191944 | tf_op jit(solution)/shard_map/ppermute | solution.py:48
  24.3 22.2 %copy-start.2 = (f32[64,512]{1,0:T(8,128)S(1)}, f32[64,512]{1,0:T(8,128)}, u32[]{:S(2)}) copy-start(f32[64,512]{1,0:T(8,128)} %refs_8_.3) | copy-start | bytes 393220
  24.3 22.2 %copy-start.3 = (f32[512,64]{0,1:T(8,128)S(1)}, f32[512,64]{0,1:T(8,128)}, u32[]{:S(2)}) copy-start(f32[512,64]{0,1:T(8,128)} %param.41) | copy-start | bytes 393220
  24.3 22.2 %copy-start.8 = (f32[64,128]{1,0:T(8,128)S(1)}, f32[64,128]{1,0:T(8,128)}, u32[]{:S(2)}) copy-start(f32[64,128]{1,0:T(8,128)} %refs_9_.3) | copy-start | bytes 98308
  24.6 7.7 %collective-permute-start.6 = (f16[776,128]{1,0:T(8,128)(2,1)S(1)}, f16[776,128]{1,0:T(8,128)(2,1)S(1)}, u32[]{:S(2)}, u32[]{:S(2)}) collective-permute-start(f16[776,128]{1,0:T(8,128)(2,1)S(1)} %get-tuple-element.101), channel_id=1, source_target_pairs={{0,64},{1,17},{2,66},{3,19},{4,68},{5,21},{6,70},{7,23},{8,72},{9,... | collective-permute-start | bytes 595976 | tf_op jit(solution)/shard_map/ppermute | solution.py:48
  28.7 6.9 %collective-permute-start.8 = (f16[776,128]{1,0:T(8,128)(2,1)S(1)}, f16[776,128]{1,0:T(8,128)(2,1)S(1)}, u32[]{:S(2)}, u32[]{:S(2)}) collective-permute-start(f16[776,128]{1,0:T(8,128)(2,1)S(1)} %get-tuple-element.102), channel_id=1, source_target_pairs={{0,96},{1,25},{2,98},{3,27},{4,100},{5,29},{6,102},{7,31},{8,104},... | collective-permute-start | bytes 595976 | tf_op jit(solution)/shard_map/ppermute | solution.py:48
  29.4 6.9 %collective-permute-start.7 = (f16[776,128]{1,0:T(8,128)(2,1)S(1)}, f16[776,128]{1,0:T(8,128)(2,1)S(1)}, u32[]{:S(2)}, u32[]{:S(2)}) collective-permute-start(f16[776,128]{1,0:T(8,128)(2,1)S(1)} %get-tuple-element.103), channel_id=1, source_target_pairs={{0,32},{1,9},{2,34},{3,11},{4,36},{5,13},{6,38},{7,15},{8,40},{9,1... | collective-permute-start | bytes 595976 | tf_op jit(solution)/shard_map/ppermute | solution.py:48
  36.7 1.2 %collective-permute-start.9 = (f32[16,128]{1,0:T(8,128)S(1)}, f32[16,128]{1,0:T(8,128)S(1)}, u32[]{:S(2)}, u32[]{:S(2)}) collective-permute-start(f32[16,128]{1,0:T(8,128)S(1)} %norms.1), channel_id=1, source_target_pairs={{0,1},{1,0},{2,3},{3,2},{4,5},{5,4},{6,7},{7,6},{8,9},{9,8},{10,11... | collective-permute-start | bytes 24584 | tf_op jit(solution)/shard_map/ppermute | solution.py:431
  37.9 3.7 %collective-permute-start.10 = (f32[16,128]{1,0:T(8,128)S(1)}, f32[16,128]{1,0:T(8,128)S(1)}, u32[]{:S(2)}, u32[]{:S(2)}) collective-permute-start(f32[16,128]{1,0:T(8,128)S(1)} %add.45), channel_id=1, source_target_pairs={{0,2},{1,3},{2,0},{3,1},{4,6},{5,7},{6,4},{7,5},{8,10},{9,11},{10,... | collective-permute-start | bytes 24584 | tf_op jit(solution)/shard_map/ppermute | solution.py:431
  41.6 4.9 %collective-permute-start.11 = (f32[16,128]{1,0:T(8,128)S(1)}, f32[16,128]{1,0:T(8,128)S(1)}, u32[]{:S(2)}, u32[]{:S(2)}) collective-permute-start(f32[16,128]{1,0:T(8,128)S(1)} %add.46), channel_id=1, source_target_pairs={{0,6},{1,7},{2,4},{3,5},{4,2},{5,3},{6,0},{7,1},{8,14},{9,15},{10,... | collective-permute-start | bytes 24584 | tf_op jit(solution)/shard_map/ppermute | solution.py:431
  46.9 7.3 %collective-permute-start.12 = (bf16[776,128]{1,0:T(8,128)(2,1)S(1)}, bf16[776,128]{1,0:T(8,128)(2,1)S(1)}, u32[]{:S(2)}, u32[]{:S(2)}) collective-permute-start(bf16[776,128]{1,0:T(8,128)(2,1)S(1)} %halves.1), channel_id=1, source_target_pairs={{0,64},{1,17},{2,66},{3,19},{4,68},{5,21},{6,70},{7,23},{8,72},{9,... | collective-permute-start | bytes 595976 | tf_op jit(solution)/shard_map/ppermute | solution.py:48
  48.7 6.8 %collective-permute-start.16 = (bf16[776,128]{1,0:T(8,128)(2,1)S(1)}, bf16[776,128]{1,0:T(8,128)(2,1)S(1)}, u32[]{:S(2)}, u32[]{:S(2)}) collective-permute-start(bf16[776,128]{1,0:T(8,128)(2,1)S(1)} %halves.1), channel_id=1, source_target_pairs={{0,96},{1,25},{2,98},{3,27},{4,100},{5,29},{6,102},{7,31},{8,104},... | collective-permute-start | bytes 595976 | tf_op jit(solution)/shard_map/ppermute | solution.py:48
  49.8 8.7 %collective-permute-start.15 = (bf16[776,128]{1,0:T(8,128)(2,1)S(1)}, bf16[776,128]{1,0:T(8,128)(2,1)S(1)}, u32[]{:S(2)}, u32[]{:S(2)}) collective-permute-start(bf16[776,128]{1,0:T(8,128)(2,1)S(1)} %halves.1), channel_id=1, source_target_pairs={{0,32},{1,9},{2,34},{3,11},{4,36},{5,13},{6,38},{7,15},{8,40},{9,1... | collective-permute-start | bytes 595976 | tf_op jit(solution)/shard_map/ppermute | solution.py:48
  54.2 7.9 %collective-permute-start.13 = (bf16[2,776,128]{2,1,0:T(8,128)(2,1)S(1)}, bf16[2,776,128]{2,1,0:T(8,128)(2,1)S(1)}, u32[]{:S(2)}, u32[]{:S(2)}) collective-permute-start(bf16[2,776,128]{2,1,0:T(8,128)(2,1)S(1)} %pad_maximum_fusion.refs_0_), channel_id=1, source_target_pairs={{0,8},{1,33},{2,10},{3,35},{4,12},{5,37},{6,14},{7,39},{8,16},{9,4... | collective-permute-start | bytes 1191944 | tf_op jit(solution)/shard_map/ppermute | solution.py:48
  58.6 9.1 %collective-permute-start.17 = (bf16[2,776,128]{2,1,0:T(8,128)(2,1)S(1)}, bf16[2,776,128]{2,1,0:T(8,128)(2,1)S(1)}, u32[]{:S(2)}, u32[]{:S(2)}) collective-permute-start(bf16[2,776,128]{2,1,0:T(8,128)(2,1)S(1)} %pad_maximum_fusion.1.refs_1_), channel_id=1, source_target_pairs={{0,24},{1,97},{2,26},{3,99},{4,28},{5,101},{6,30},{7,103},{8,0},{9... | collective-permute-start | bytes 1191944 | tf_op jit(solution)/shard_map/ppermute | solution.py:48
  58.7 13.3 %collective-permute-start.20 = (bf16[2,776,128]{2,1,0:T(8,128)(2,1)S(1)}, bf16[2,776,128]{2,1,0:T(8,128)(2,1)S(1)}, u32[]{:S(2)}, u32[]{:S(2)}) collective-permute-start(bf16[2,776,128]{2,1,0:T(8,128)(2,1)S(1)} %pad_maximum_fusion.refs_0_), channel_id=1, source_target_pairs={{0,24},{1,97},{2,26},{3,99},{4,28},{5,101},{6,30},{7,103},{8,0},{9... | collective-permute-start | bytes 1191944 | tf_op jit(solution)/shard_map/ppermute | solution.py:48
  59.2 12.8 %collective-permute-start.19 = (bf16[2,776,128]{2,1,0:T(8,128)(2,1)S(1)}, bf16[2,776,128]{2,1,0:T(8,128)(2,1)S(1)}, u32[]{:S(2)}, u32[]{:S(2)}) collective-permute-start(bf16[2,776,128]{2,1,0:T(8,128)(2,1)S(1)} %pad_maximum_fusion.1.refs_1_), channel_id=1, source_target_pairs={{0,8},{1,33},{2,10},{3,35},{4,12},{5,37},{6,14},{7,39},{8,16},{9,4... | collective-permute-start | bytes 1191944 | tf_op jit(solution)/shard_map/ppermute | solution.py:48
  62.1 12.4 %collective-permute-start.14 = (bf16[2,776,128]{2,1,0:T(8,128)(2,1)S(1)}, bf16[2,776,128]{2,1,0:T(8,128)(2,1)S(1)}, u32[]{:S(2)}, u32[]{:S(2)}) collective-permute-start(bf16[2,776,128]{2,1,0:T(8,128)(2,1)S(1)} %collective-permute-done.13.refs_2_), channel_id=1, source_target_pairs={{0,8},{1,33},{2,10},{3,35},{4,12},{5,37},{6,14},{7,39},{8,16},{9,4... | collective-permute-start | bytes 1191944 | tf_op jit(solution)/shard_map/ppermute | solution.py:48
  67.7 9.0 %collective-permute-start.18 = (bf16[2,776,128]{2,1,0:T(8,128)(2,1)S(1)}, bf16[2,776,128]{2,1,0:T(8,128)(2,1)S(1)}, u32[]{:S(2)}, u32[]{:S(2)}) collective-permute-start(bf16[2,776,128]{2,1,0:T(8,128)(2,1)S(1)} %collective-permute-done.17.refs_5_), channel_id=1, source_target_pairs={{0,24},{1,97},{2,26},{3,99},{4,28},{5,101},{6,30},{7,103},{8,0},{9... | collective-permute-start | bytes 1191944 | tf_op jit(solution)/shard_map/ppermute | solution.py:48
  (13 other events, 228.5 us)

commit v3 on v2

--- a/solution.py
+++ b/solution.py
@@ -202,22 +202,25 @@
         table = jnp.where(lane == m, o, jnp.where(lane == 8 + m, s, table))
     table = jnp.concatenate([table, jnp.zeros((128 - B, 128), jnp.float32)], axis=0)
     table = table.T[:16, :]
-    part[...] = table
-
-
-def norms(total, *params):
+    for r in range(part.shape[0]):
+        part[r] = table
+
+
+def norms(copies, total, *params):
     return pl.pallas_call(
         norms_kernel,
         in_specs=[VM] * 7,
         out_specs=VM,
-        out_shape=pltpu.VMEM((16, 128), jnp.float32),
+        out_shape=pltpu.VMEM((copies, 16, 128), jnp.float32),
         compiler_params=PARAMS,
         name="norms",
     )(vmem(total), *params)
 
 
 def steps(parts, total, params, states, store, store_half):
-    sums = parts[...]
+    sums = parts[0]
+    for d in range(1, parts.shape[0]):
+        sums = sums + parts[d]
     ratio = jnp.sqrt(sums[:8]) * lax.rsqrt(sums[8:16] + 1e-06)
     ratio = jnp.concatenate([ratio, jnp.zeros((120, 128), jnp.float32)], axis=0).T[:B, :]
 
@@ -426,9 +429,8 @@
     four = turn(place, four_a, four_b)
     total = four[0] + sum(marked(four[e].astype(f16), e).astype(f32) for e in ORDER[1:])
 
-    parts = norms(total, *params[:6])
-    for partner in (lambda m: m ^ 1, lambda m: m ^ 2, lambda m: m ^ 6):
-        parts = parts + lax.ppermute(parts, "model", [(m, partner(m)) for m in range(8)])
+    part = norms(lax.axis_size("model"), total, *params[:6])
+    parts = lax.all_to_all(part, "model", 0, 0, tiled=True)
     half = halves(parts, total, params, states)
 
     row = [half] + [marked(half, e) for e in ORDER[1:]]

time: 79.6 us -> 77.8 us (0.977)
  blocking collectives: 0 us -> 9.71 us
  waiting for transfers between devices: 35.6 us -> 28.8 us
  starting transfers between devices: 27.3 us -> 22.5 us
    all_to_all x0 -> x1, blocking collectives: none -> 9.71 us  [local(): parts = lax.all_to_all(part, 'model', 0, 0, tiled=True)]
    ppermute x3 -> x0, waiting for transfers between devices: 5.42 us -> none  [local(): lax.ppermute(parts, 'model', [(m, partner(m)) for m in range(8)])]
    ppermute x3 -> x0, starting transfers between devices: 4.29 us -> none  [local(): lax.ppermute(parts, 'model', [(m, partner(m)) for m in range(8)])]
    ppermute x18, waiting for transfers between devices: 30.2 us -> 28.8 us  [send(): return lax.ppermute(x, ('replica', 'model'), pairs)]
  transfers between devices with their start and end apart: 21 -> 18, of which waited for: 18 -> 15; matrix products, arithmetic and copies ran while one was open for 1% -> 1% of each run, Pallas kernels for 8% -> 8%
where the time goes in v3:
time: 77.8 us; the launch traced here: 77.6 us
  waiting for transfers between devices  28.8 us (37%)
  starting transfers between devices  22.5 us (29%)
  Pallas kernels  13.2 us (17%)
  blocking collectives  9.71 us (12%)
  other arithmetic  1.58 us (2%)
  between operations  1.05 us (1%)
  local copies, waits for them, and re-layouts  0.81 us (1%)
    ppermute x18, waiting for transfers between devices, send(): return lax.ppermute(x, ('replica', 'model'), pairs)  28.8 us
    ppermute x18, starting transfers between devices, send(): return lax.ppermute(x, ('replica', 'model'), pairs)  22.5 us
    all_to_all x1, blocking collectives, local(): parts = lax.all_to_all(part, 'model', 0, 0, tiled=True)  9.71 us
    pallas_call x2, Pallas kernels, pack(): pl.pallas_call(kernel, in_specs=[SM] + [HB] * 8, out_specs=(VM, VM), out_...  6.04 us
    pallas_call x1, Pallas kernels, unpack(): pl.pallas_call(early_kernel, in_specs=[SM] + [VM] * 6, out_specs=(*[HB] *...  2.46 us
    pallas_call x1, Pallas kernels, unpack(): pl.pallas_call(late_kernel, in_specs=[SM, VM, VM] + [HB] * 4 + [VM] * 3,...  2.1 us
  transfers between devices with their start and end apart: 18, of which 15 were waited for; matrix products, arithmetic and copies ran while one was open for 1% of the time, Pallas kernels for 8%

profile of v3, /device:TPU:24, one launch (start us, length us, event | category | flops | bytes accessed | tf_op | source)
XLA Modules:
  0.0 77.6 jit_solution(771803997137670527)
XLA Ops:
  0.7 3.4 %shard_map.415 = (f32[3,4,192,256]{3,2,1,0:T(8,128)S(1)}, f32[3,776,256]{2,1,0:T(8,128)S(1)}) custom-call(s32[3]{0:T(128)S(1)} %pad_add_fusion.at_ref, f32[4,4,64,512]{3,2,1,0:T(8,128)} %bitcast.90, f32[4,4,64,128]{3,2,1,0:T(8,128)} %bitcast.92, f32[4,4,64,128]{3,2,1,0:T(8,128)} %bitcast.94, f32[1024,128]{1,0:T(8,128)} %bitcast.96, f32[1,512,1024]{2,1,0:T(8,128)} %down.3, ...), custom_call_target="tpu_custom_call" | custom-call | tf_op jit(solution)/shard_map/pallas_call | solution.py:141
  4.8 2.0 %collective-permute-start.1 = (f16[776,256]{1,0:T(8,128)(2,1)S(1)}, f16[776,256]{1,0:T(8,128)(2,1)S(1)}, u32[]{:S(2)}, u32[]{:S(2)}) collective-permute-start(f16[776,256]{1,0:T(8,128)(2,1)S(1)} %get-tuple-element.97), channel_id=1, source_target_pairs={{0,24},{1,97},{2,26},{3,99},{4,28},{5,101},{6,30},{7,103},{8,0},{9... | collective-permute-start | bytes 1191944 | tf_op jit(solution)/shard_map/ppermute | solution.py:48
  7.5 2.5 %collective-permute-start.4 = (f16[776,256]{1,0:T(8,128)(2,1)S(1)}, f16[776,256]{1,0:T(8,128)(2,1)S(1)}, u32[]{:S(2)}, u32[]{:S(2)}) collective-permute-start(f16[776,256]{1,0:T(8,128)(2,1)S(1)} %get-tuple-element.96), channel_id=1, source_target_pairs={{0,8},{1,33},{2,10},{3,35},{4,12},{5,37},{6,14},{7,39},{8,16},{9,4... | collective-permute-start | bytes 1191944 | tf_op jit(solution)/shard_map/ppermute | solution.py:48
  10.0 2.3 %collective-permute-done = f16[768,256]{1,0:T(8,128)(2,1)S(1)} collective-permute-done((f16[768,256]{1,0:T(8,128)(2,1)S(1)}, f16[768,256]{1,0:T(8,128)(2,1)S(1)}, u32[]{:S(2)}, u32[]{:S(2)}) %collective-permute-start) | collective-permute-done | bytes 393248 | tf_op jit(solution)/shard_map/ppermute | solution.py:48
  12.4 1.4 %collective-permute-start.3 = (f16[768,256]{1,0:T(8,128)(2,1)S(1)}, f16[768,256]{1,0:T(8,128)(2,1)S(1)}, u32[]{:S(2)}, u32[]{:S(2)}) collective-permute-start(f16[768,256]{1,0:T(8,128)(2,1)S(1)} %fusion.7), channel_id=1, source_target_pairs={{0,8},{1,33},{2,10},{3,35},{4,12},{5,37},{6,14},{7,39},{8,16},{9,4... | collective-permute-start | bytes 1179656 | tf_op jit(solution)/shard_map/ppermute | solution.py:48
  14.8 2.7 %shard_map.416 = (f32[1,4,192,256]{3,2,1,0:T(8,128)S(1)}, f32[1,776,256]{2,1,0:T(8,128)S(1)}) custom-call(s32[3]{0:T(128)S(1)} %pad_add_fusion.at_ref, f32[4,4,64,512]{3,2,1,0:T(8,128)} %bitcast.91, f32[4,4,64,128]{3,2,1,0:T(8,128)} %bitcast.93, f32[4,4,64,128]{3,2,1,0:T(8,128)} %bitcast.95, f32[1024,128]{1,0:T(8,128)} %bitcast.97, f32[1,512,1024]{2,1,0:T(8,128)} %down.3, ...), custom_call_target="tpu_custom_call" | custom-call | tf_op jit(solution)/shard_map/pallas_call | solution.py:141
  18.1 2.6 %collective-permute-done.3 = f16[768,256]{1,0:T(8,128)(2,1)S(1)} collective-permute-done((f16[768,256]{1,0:T(8,128)(2,1)S(1)}, f16[768,256]{1,0:T(8,128)(2,1)S(1)}, u32[]{:S(2)}, u32[]{:S(2)}) %collective-permute-start.3) | collective-permute-done | bytes 393248 | tf_op jit(solution)/shard_map/ppermute | solution.py:48
  20.9 2.2 %collective-permute-done.5 = f16[776,256]{1,0:T(8,128)(2,1)S(1)} collective-permute-done((f16[776,256]{1,0:T(8,128)(2,1)S(1)}, f16[776,256]{1,0:T(8,128)(2,1)S(1)}, u32[]{:S(2)}, u32[]{:S(2)}) %collective-permute-start.5) | collective-permute-done | bytes 397344 | tf_op jit(solution)/shard_map/ppermute | solution.py:48
  24.6 4.1 %collective-permute-start.6 = (f16[776,128]{1,0:T(8,128)(2,1)S(1)}, f16[776,128]{1,0:T(8,128)(2,1)S(1)}, u32[]{:S(2)}, u32[]{:S(2)}) collective-permute-start(f16[776,128]{1,0:T(8,128)(2,1)S(1)} %get-tuple-element.101), channel_id=1, source_target_pairs={{0,64},{1,17},{2,66},{3,19},{4,68},{5,21},{6,70},{7,23},{8,72},{9,... | collective-permute-start | bytes 595976 | tf_op jit(solution)/shard_map/ppermute | solution.py:48
  29.4 1.3 %collective-permute-start.7 = (f16[776,128]{1,0:T(8,128)(2,1)S(1)}, f16[776,128]{1,0:T(8,128)(2,1)S(1)}, u32[]{:S(2)}, u32[]{:S(2)}) collective-permute-start(f16[776,128]{1,0:T(8,128)(2,1)S(1)} %get-tuple-element.103), channel_id=1, source_target_pairs={{0,32},{1,9},{2,34},{3,11},{4,36},{5,13},{6,38},{7,15},{8,40},{9,1... | collective-permute-start | bytes 595976 | tf_op jit(solution)/shard_map/ppermute | solution.py:48
  30.7 1.6 %collective-permute-done.6 = f16[776,128]{1,0:T(8,128)(2,1)S(1)} collective-permute-done((f16[776,128]{1,0:T(8,128)(2,1)S(1)}, f16[776,128]{1,0:T(8,128)(2,1)S(1)}, u32[]{:S(2)}, u32[]{:S(2)}) %collective-permute-start.6) | collective-permute-done | bytes 198688 | tf_op jit(solution)/shard_map/ppermute | solution.py:48
  32.4 3.2 %collective-permute-done.8 = f16[776,128]{1,0:T(8,128)(2,1)S(1)} collective-permute-done((f16[776,128]{1,0:T(8,128)(2,1)S(1)}, f16[776,128]{1,0:T(8,128)(2,1)S(1)}, u32[]{:S(2)}, u32[]{:S(2)}) %collective-permute-start.8) | collective-permute-done | bytes 198688 | tf_op jit(solution)/shard_map/ppermute | solution.py:48
  36.7 9.7 %all_to_all.5.parts = f32[8,16,128]{2,1,0:T(8,128)S(1)} all-to-all(f32[8,16,128]{2,1,0:T(8,128)S(1)} %norms.1), channel_id=1, replica_groups=mesh['replica'=16,'model'=8] {'model'}, dimensions={0} | all-to-all | bytes 131072 | tf_op jit(solution)/shard_map/all_to_all | solution.py:433
  46.9 1.8 %collective-permute-start.9 = (bf16[776,128]{1,0:T(8,128)(2,1)S(1)}, bf16[776,128]{1,0:T(8,128)(2,1)S(1)}, u32[]{:S(2)}, u32[]{:S(2)}) collective-permute-start(bf16[776,128]{1,0:T(8,128)(2,1)S(1)} %halves.1), channel_id=1, source_target_pairs={{0,64},{1,17},{2,66},{3,19},{4,68},{5,21},{6,70},{7,23},{8,72},{9,... | collective-permute-start | bytes 595976 | tf_op jit(solution)/shard_map/ppermute | solution.py:48
  50.7 3.5 %collective-permute-done.9 = bf16[776,128]{1,0:T(8,128)(2,1)S(1)} collective-permute-done((bf16[776,128]{1,0:T(8,128)(2,1)S(1)}, bf16[776,128]{1,0:T(8,128)(2,1)S(1)}, u32[]{:S(2)}, u32[]{:S(2)}) %collective-permute-start.9) | collective-permute-done | bytes 198688 | tf_op jit(solution)/shard_map/ppermute | solution.py:48
  55.5 1.3 %collective-permute-done.12 = bf16[776,128]{1,0:T(8,128)(2,1)S(1)} collective-permute-done((bf16[776,128]{1,0:T(8,128)(2,1)S(1)}, bf16[776,128]{1,0:T(8,128)(2,1)S(1)}, u32[]{:S(2)}, u32[]{:S(2)}) %collective-permute-start.12) | collective-permute-done | bytes 198688 | tf_op jit(solution)/shard_map/ppermute | solution.py:48
  57.4 2.8 %collective-permute-start.16 = (bf16[2,776,128]{2,1,0:T(8,128)(2,1)S(1)}, bf16[2,776,128]{2,1,0:T(8,128)(2,1)S(1)}, u32[]{:S(2)}, u32[]{:S(2)}) collective-permute-start(bf16[2,776,128]{2,1,0:T(8,128)(2,1)S(1)} %pad_maximum_fusion.1.refs_1_), channel_id=1, source_target_pairs={{0,8},{1,33},{2,10},{3,35},{4,12},{5,37},{6,14},{7,39},{8,16},{9,4... | collective-permute-start | bytes 1191944 | tf_op jit(solution)/shard_map/ppermute | solution.py:48
  60.2 1.9 %collective-permute-done.10.refs_2_ = bf16[2,776,128]{2,1,0:T(8,128)(2,1)S(1)} collective-permute-done((bf16[2,776,128]{2,1,0:T(8,128)(2,1)S(1)}, bf16[2,776,128]{2,1,0:T(8,128)(2,1)S(1)}, u32[]{:S(2)}, u32[]{:S(2)}) %collective-permute-start.10) | collective-permute-done | bytes 397344 | tf_op jit(solution)/shard_map/ppermute | solution.py:48
  62.1 1.4 %collective-permute-start.11 = (bf16[2,776,128]{2,1,0:T(8,128)(2,1)S(1)}, bf16[2,776,128]{2,1,0:T(8,128)(2,1)S(1)}, u32[]{:S(2)}, u32[]{:S(2)}) collective-permute-start(bf16[2,776,128]{2,1,0:T(8,128)(2,1)S(1)} %collective-permute-done.10.refs_2_), channel_id=1, source_target_pairs={{0,8},{1,33},{2,10},{3,35},{4,12},{5,37},{6,14},{7,39},{8,16},{9,4... | collective-permute-start | bytes 1191944 | tf_op jit(solution)/shard_map/ppermute | solution.py:48
  63.4 2.4 %collective-permute-done.14.refs_5_ = bf16[2,776,128]{2,1,0:T(8,128)(2,1)S(1)} collective-permute-done((bf16[2,776,128]{2,1,0:T(8,128)(2,1)S(1)}, bf16[2,776,128]{2,1,0:T(8,128)(2,1)S(1)}, u32[]{:S(2)}, u32[]{:S(2)}) %collective-permute-start.14) | collective-permute-done | bytes 397344 | tf_op jit(solution)/shard_map/ppermute | solution.py:48
  67.0 3.1 %collective-permute-done.17.refs_4_ = bf16[2,776,128]{2,1,0:T(8,128)(2,1)S(1)} collective-permute-done((bf16[2,776,128]{2,1,0:T(8,128)(2,1)S(1)}, bf16[2,776,128]{2,1,0:T(8,128)(2,1)S(1)}, u32[]{:S(2)}, u32[]{:S(2)}) %collective-permute-start.17) | collective-permute-done | bytes 397344 | tf_op jit(solution)/shard_map/ppermute | solution.py:48
  70.1 2.5 %unpack_early.1 = (bf16[1024,512]{1,0:T(8,128)(2,1)}, bf16[1024,128]{1,0:T(8,128)(2,1)}, bf16[1024,128]{1,0:T(8,128)(2,1)}, bf16[1024,128]{1,0:T(8,128)(2,1)}, b...) custom-call(s32[3]{0:T(128)S(1)} %pad_add_fusion.at_ref, ...), custom_call_target="tpu_custom_call" | custom-call | tf_op jit(solution)/shard_map/unpack_early/pallas_call | solution.py:370
  72.6 2.3 %collective-permute-done.15.b = bf16[2,776,128]{2,1,0:T(8,128)(2,1)S(1)} collective-permute-done((bf16[2,776,128]{2,1,0:T(8,128)(2,1)S(1)}, bf16[2,776,128]{2,1,0:T(8,128)(2,1)S(1)}, u32[]{:S(2)}, u32[]{:S(2)}) %collective-permute-start.15) | collective-permute-done | bytes 397344 | tf_op jit(solution)/shard_map/ppermute | solution.py:48
  74.9 2.1 %unpack_late.1 = (bf16[1024,512]{1,0:T(8,128)(2,1)}, bf16[1024,128]{1,0:T(8,128)(2,1)}, bf16[1024,128]{1,0:T(8,128)(2,1)}, bf16[1024,128]{1,0:T(8,128)(2,1)}, bf...) custom-call(s32[3]{0:T(128)S(1)} %pad_add_fusion.at_ref, ...), custom_call_target="tpu_custom_call", output_to_operand_aliasing={{0}: (3, {}), {1}: (4, {}), {2}: (5, {}), {3}: (6, {}), {4}... | custom-call | tf_op jit(solution)/shard_map/unpack_late/pallas_call | solution.py:383
  (68 shorter events, 12.6 us)
Async XLA Ops:
  4.4 7.8 %collective-permute-start = (f16[768,256]{1,0:T(8,128)(2,1)S(1)}, f16[768,256]{1,0:T(8,128)(2,1)S(1)}, u32[]{:S(2)}, u32[]{:S(2)}) collective-permute-start(f16[768,256]{1,0:T(8,128)(2,1)S(1)} %bitcast.99), channel_id=1, source_target_pairs={{0,8},{1,33},{2,10},{3,35},{4,12},{5,37},{6,14},{7,39},{8,16},{9,4... | collective-permute-start | bytes 1179656 | tf_op jit(solution)/shard_map/ppermute | solution.py:48
  4.8 9.1 %collective-permute-start.1 = (f16[776,256]{1,0:T(8,128)(2,1)S(1)}, f16[776,256]{1,0:T(8,128)(2,1)S(1)}, u32[]{:S(2)}, u32[]{:S(2)}) collective-permute-start(f16[776,256]{1,0:T(8,128)(2,1)S(1)} %get-tuple-element.97), channel_id=1, source_target_pairs={{0,24},{1,97},{2,26},{3,99},{4,28},{5,101},{6,30},{7,103},{8,0},{9... | collective-permute-start | bytes 1191944 | tf_op jit(solution)/shard_map/ppermute | solution.py:48
  6.7 11.3 %collective-permute-start.2 = (f16[768,256]{1,0:T(8,128)(2,1)S(1)}, f16[768,256]{1,0:T(8,128)(2,1)S(1)}, u32[]{:S(2)}, u32[]{:S(2)}) collective-permute-start(f16[768,256]{1,0:T(8,128)(2,1)S(1)} %bitcast.98), channel_id=1, source_target_pairs={{0,24},{1,97},{2,26},{3,99},{4,28},{5,101},{6,30},{7,103},{8,0},{9... | collective-permute-start | bytes 1179656 | tf_op jit(solution)/shard_map/ppermute | solution.py:48
  7.5 13.4 %collective-permute-start.4 = (f16[776,256]{1,0:T(8,128)(2,1)S(1)}, f16[776,256]{1,0:T(8,128)(2,1)S(1)}, u32[]{:S(2)}, u32[]{:S(2)}) collective-permute-start(f16[776,256]{1,0:T(8,128)(2,1)S(1)} %get-tuple-element.96), channel_id=1, source_target_pairs={{0,8},{1,33},{2,10},{3,35},{4,12},{5,37},{6,14},{7,39},{8,16},{9,4... | collective-permute-start | bytes 1191944 | tf_op jit(solution)/shard_map/ppermute | solution.py:48
  12.4 8.3 %collective-permute-start.3 = (f16[768,256]{1,0:T(8,128)(2,1)S(1)}, f16[768,256]{1,0:T(8,128)(2,1)S(1)}, u32[]{:S(2)}, u32[]{:S(2)}) collective-permute-start(f16[768,256]{1,0:T(8,128)(2,1)S(1)} %fusion.7), channel_id=1, source_target_pairs={{0,8},{1,33},{2,10},{3,35},{4,12},{5,37},{6,14},{7,39},{8,16},{9,4... | collective-permute-start | bytes 1179656 | tf_op jit(solution)/shard_map/ppermute | solution.py:48
  14.0 9.1 %collective-permute-start.5 = (f16[776,256]{1,0:T(8,128)(2,1)S(1)}, f16[776,256]{1,0:T(8,128)(2,1)S(1)}, u32[]{:S(2)}, u32[]{:S(2)}) collective-permute-start(f16[776,256]{1,0:T(8,128)(2,1)S(1)} %fusion.3), channel_id=1, source_target_pairs={{0,24},{1,97},{2,26},{3,99},{4,28},{5,101},{6,30},{7,103},{8,0},{9... | collective-permute-start | bytes 1191944 | tf_op jit(solution)/shard_map/ppermute | solution.py:48
  24.4 22.1 %copy-start.2 = (f32[64,512]{1,0:T(8,128)S(1)}, f32[64,512]{1,0:T(8,128)}, u32[]{:S(2)}) copy-start(f32[64,512]{1,0:T(8,128)} %refs_8_.3) | copy-start | bytes 393220
  24.4 22.1 %copy-start.3 = (f32[512,64]{0,1:T(8,128)S(1)}, f32[512,64]{0,1:T(8,128)}, u32[]{:S(2)}) copy-start(f32[512,64]{0,1:T(8,128)} %param.41) | copy-start | bytes 393220
  24.4 22.1 %copy-start.8 = (f32[64,128]{1,0:T(8,128)S(1)}, f32[64,128]{1,0:T(8,128)}, u32[]{:S(2)}) copy-start(f32[64,128]{1,0:T(8,128)} %refs_9_.3) | copy-start | bytes 98308
  24.4 22.0 %copy-start.9 = (f32[64,128]{1,0:T(8,128)S(1)}, f32[64,128]{1,0:T(8,128)}, u32[]{:S(2)}) copy-start(f32[64,128]{1,0:T(8,128)} %refs_10_.3) | copy-start | bytes 98308
  24.4 22.0 %copy-start.10 = (f32[64,128]{1,0:T(8,128)S(1)}, f32[64,128]{1,0:T(8,128)}, u32[]{:S(2)}) copy-start(f32[64,128]{1,0:T(8,128)} %refs_11_.3) | copy-start | bytes 98308
  24.4 22.0 %copy-start.11 = (f32[128,64]{0,1:T(8,128)S(1)}, f32[128,64]{0,1:T(8,128)}, u32[]{:S(2)}) copy-start(f32[128,64]{0,1:T(8,128)} %param.45) | copy-start | bytes 98308
  24.6 7.7 %collective-permute-start.6 = (f16[776,128]{1,0:T(8,128)(2,1)S(1)}, f16[776,128]{1,0:T(8,128)(2,1)S(1)}, u32[]{:S(2)}, u32[]{:S(2)}) collective-permute-start(f16[776,128]{1,0:T(8,128)(2,1)S(1)} %get-tuple-element.101), channel_id=1, source_target_pairs={{0,64},{1,17},{2,66},{3,19},{4,68},{5,21},{6,70},{7,23},{8,72},{9,... | collective-permute-start | bytes 595976 | tf_op jit(solution)/shard_map/ppermute | solution.py:48
  28.7 6.9 %collective-permute-start.8 = (f16[776,128]{1,0:T(8,128)(2,1)S(1)}, f16[776,128]{1,0:T(8,128)(2,1)S(1)}, u32[]{:S(2)}, u32[]{:S(2)}) collective-permute-start(f16[776,128]{1,0:T(8,128)(2,1)S(1)} %get-tuple-element.102), channel_id=1, source_target_pairs={{0,96},{1,25},{2,98},{3,27},{4,100},{5,29},{6,102},{7,31},{8,104},... | collective-permute-start | bytes 595976 | tf_op jit(solution)/shard_map/ppermute | solution.py:48
  29.4 6.9 %collective-permute-start.7 = (f16[776,128]{1,0:T(8,128)(2,1)S(1)}, f16[776,128]{1,0:T(8,128)(2,1)S(1)}, u32[]{:S(2)}, u32[]{:S(2)}) collective-permute-start(f16[776,128]{1,0:T(8,128)(2,1)S(1)} %get-tuple-element.103), channel_id=1, source_target_pairs={{0,32},{1,9},{2,34},{3,11},{4,36},{5,13},{6,38},{7,15},{8,40},{9,1... | collective-permute-start | bytes 595976 | tf_op jit(solution)/shard_map/ppermute | solution.py:48
  46.9 7.3 %collective-permute-start.9 = (bf16[776,128]{1,0:T(8,128)(2,1)S(1)}, bf16[776,128]{1,0:T(8,128)(2,1)S(1)}, u32[]{:S(2)}, u32[]{:S(2)}) collective-permute-start(bf16[776,128]{1,0:T(8,128)(2,1)S(1)} %halves.1), channel_id=1, source_target_pairs={{0,64},{1,17},{2,66},{3,19},{4,68},{5,21},{6,70},{7,23},{8,72},{9,... | collective-permute-start | bytes 595976 | tf_op jit(solution)/shard_map/ppermute | solution.py:48
  48.7 6.8 %collective-permute-start.13 = (bf16[776,128]{1,0:T(8,128)(2,1)S(1)}, bf16[776,128]{1,0:T(8,128)(2,1)S(1)}, u32[]{:S(2)}, u32[]{:S(2)}) collective-permute-start(bf16[776,128]{1,0:T(8,128)(2,1)S(1)} %halves.1), channel_id=1, source_target_pairs={{0,96},{1,25},{2,98},{3,27},{4,100},{5,29},{6,102},{7,31},{8,104},... | collective-permute-start | bytes 595976 | tf_op jit(solution)/shard_map/ppermute | solution.py:48
  49.8 6.9 %collective-permute-start.12 = (bf16[776,128]{1,0:T(8,128)(2,1)S(1)}, bf16[776,128]{1,0:T(8,128)(2,1)S(1)}, u32[]{:S(2)}, u32[]{:S(2)}) collective-permute-start(bf16[776,128]{1,0:T(8,128)(2,1)S(1)} %halves.1), channel_id=1, source_target_pairs={{0,32},{1,9},{2,34},{3,11},{4,36},{5,13},{6,38},{7,15},{8,40},{9,1... | collective-permute-start | bytes 595976 | tf_op jit(solution)/shard_map/ppermute | solution.py:48
  54.2 7.9 %collective-permute-start.10 = (bf16[2,776,128]{2,1,0:T(8,128)(2,1)S(1)}, bf16[2,776,128]{2,1,0:T(8,128)(2,1)S(1)}, u32[]{:S(2)}, u32[]{:S(2)}) collective-permute-start(bf16[2,776,128]{2,1,0:T(8,128)(2,1)S(1)} %pad_maximum_fusion.refs_0_), channel_id=1, source_target_pairs={{0,8},{1,33},{2,10},{3,35},{4,12},{5,37},{6,14},{7,39},{8,16},{9,4... | collective-permute-start | bytes 1191944 | tf_op jit(solution)/shard_map/ppermute | solution.py:48
  56.8 9.1 %collective-permute-start.14 = (bf16[2,776,128]{2,1,0:T(8,128)(2,1)S(1)}, bf16[2,776,128]{2,1,0:T(8,128)(2,1)S(1)}, u32[]{:S(2)}, u32[]{:S(2)}) collective-permute-start(bf16[2,776,128]{2,1,0:T(8,128)(2,1)S(1)} %pad_maximum_fusion.1.refs_1_), channel_id=1, source_target_pairs={{0,24},{1,97},{2,26},{3,99},{4,28},{5,101},{6,30},{7,103},{8,0},{9... | collective-permute-start | bytes 1191944 | tf_op jit(solution)/shard_map/ppermute | solution.py:48
  56.8 13.3 %collective-permute-start.17 = (bf16[2,776,128]{2,1,0:T(8,128)(2,1)S(1)}, bf16[2,776,128]{2,1,0:T(8,128)(2,1)S(1)}, u32[]{:S(2)}, u32[]{:S(2)}) collective-permute-start(bf16[2,776,128]{2,1,0:T(8,128)(2,1)S(1)} %pad_maximum_fusion.refs_0_), channel_id=1, source_target_pairs={{0,24},{1,97},{2,26},{3,99},{4,28},{5,101},{6,30},{7,103},{8,0},{9... | collective-permute-start | bytes 1191944 | tf_op jit(solution)/shard_map/ppermute | solution.py:48
  57.4 12.8 %collective-permute-start.16 = (bf16[2,776,128]{2,1,0:T(8,128)(2,1)S(1)}, bf16[2,776,128]{2,1,0:T(8,128)(2,1)S(1)}, u32[]{:S(2)}, u32[]{:S(2)}) collective-permute-start(bf16[2,776,128]{2,1,0:T(8,128)(2,1)S(1)} %pad_maximum_fusion.1.refs_1_), channel_id=1, source_target_pairs={{0,8},{1,33},{2,10},{3,35},{4,12},{5,37},{6,14},{7,39},{8,16},{9,4... | collective-permute-start | bytes 1191944 | tf_op jit(solution)/shard_map/ppermute | solution.py:48
  62.1 10.5 %collective-permute-start.11 = (bf16[2,776,128]{2,1,0:T(8,128)(2,1)S(1)}, bf16[2,776,128]{2,1,0:T(8,128)(2,1)S(1)}, u32[]{:S(2)}, u32[]{:S(2)}) collective-permute-start(bf16[2,776,128]{2,1,0:T(8,128)(2,1)S(1)} %collective-permute-done.10.refs_2_), channel_id=1, source_target_pairs={{0,8},{1,33},{2,10},{3,35},{4,12},{5,37},{6,14},{7,39},{8,16},{9,4... | collective-permute-start | bytes 1191944 | tf_op jit(solution)/shard_map/ppermute | solution.py:48
  65.9 9.0 %collective-permute-start.15 = (bf16[2,776,128]{2,1,0:T(8,128)(2,1)S(1)}, bf16[2,776,128]{2,1,0:T(8,128)(2,1)S(1)}, u32[]{:S(2)}, u32[]{:S(2)}) collective-permute-start(bf16[2,776,128]{2,1,0:T(8,128)(2,1)S(1)} %collective-permute-done.14.refs_5_), channel_id=1, source_target_pairs={{0,24},{1,97},{2,26},{3,99},{4,28},{5,101},{6,30},{7,103},{8,0},{9... | collective-permute-start | bytes 1191944 | tf_op jit(solution)/shard_map/ppermute | solution.py:48
  (10 other events, 161.6 us)

commit v4 on v3

--- a/solution.py
+++ b/solution.py
@@ -21,6 +21,8 @@
 SCALE = 8192.0
 SCALE_VEC = 4096.0
 ORDER = (0, 2, 1, 3)
+
+GATHER = (0, 2, 3, 1)
 
 
 def vmem(x):
@@ -295,10 +297,10 @@
     stacks = {0: refs[0:2], 1: refs[2:4], 3: refs[4:6]}
     up, query, key, value, down_s, mixed_s, vectors, up_s, query_s, key_s, value_s, rest_s, sems = refs[6:]
     for d in range(4):
-        for k, e in enumerate(ORDER):
+        for k, e in enumerate(GATHER):
             r = block_of(at_ref, (at_ref[0] - d) & 3, (at_ref[1] - e) & 3)
             rows = pl.ds(pl.multiple_of(r * B, B), B)
-            block = stacks[d][k // 2][k % 2] if d != 2 else jnp.zeros((T, 128), jnp.bfloat16)
+            block = stacks[d][k // 3][k % 3] if d != 2 else jnp.zeros((T, 128), jnp.bfloat16)
             for c in range(4):
                 up_s[rows, c * 128 : c * 128 + 128] = block[c * B : c * B + B, :]
             query_s[rows, :] = block[4 * B : 5 * B, :]
@@ -335,8 +337,8 @@
         copies[-1].start()
 
     half = lax.broadcasted_iota(jnp.int32, (128, 128), 1) >> 6
-    for i, e in enumerate(ORDER):
-        block = (a, b)[i // 2].at[i % 2]
+    for i, e in enumerate(GATHER):
+        block = (a, b)[i // 3].at[i % 3]
         r = block_of(at_ref, (at_ref[0] - 2) & 3, (at_ref[1] - e) & 3)
         rows = pl.ds(pl.multiple_of(r * B, B), B)
         for c in range(4):
@@ -433,8 +435,8 @@
     parts = lax.all_to_all(part, "model", 0, 0, tiled=True)
     half = halves(parts, total, params, states)
 
-    row = [half] + [marked(half, e) for e in ORDER[1:]]
-    own_a, own_b = jnp.stack(row[:2]), jnp.stack(row[2:])
+    row = [half] + [marked(half, e) for e in GATHER[1:]]
+    own_a, own_b = jnp.stack(row[:3]), row[3][None]
     one_a, three_a = marked(own_a, 1, 0), marked(own_a, 3, 0)
     three_b, one_b = marked(own_b, 3, 0), marked(own_b, 1, 0)
     two_a, two_b = send(one_a, 0, 1), send(three_b, 0, 3)

time: 77.8 us -> 87.1 us (1.12)
  the two profiles are of different devices: /device:TPU:24 before, /device:TPU:1 now
where the time goes in v4:
time: 87.1 us; the launch traced here: 86.9 us
  waiting for transfers between devices  32.7 us (38%)
  starting transfers between devices  25 us (29%)
  Pallas kernels  13.2 us (15%)
  blocking collectives  12.6 us (14%)
  other arithmetic  1.54 us (2%)
  between operations  1.09 us (1%)
    ppermute x18, waiting for transfers between devices, send(): return lax.ppermute(x, ('replica', 'model'), pairs)  32.7 us
    ppermute x18, starting transfers between devices, send(): return lax.ppermute(x, ('replica', 'model'), pairs)  25 us
    all_to_all x1, blocking collectives, local(): parts = lax.all_to_all(part, 'model', 0, 0, tiled=True)  12.6 us
    pallas_call x2, Pallas kernels, pack(): pl.pallas_call(kernel, in_specs=[SM] + [HB] * 8, out_specs=(VM, VM), out_...  6.04 us
    pallas_call x1, Pallas kernels, unpack(): pl.pallas_call(early_kernel, in_specs=[SM] + [VM] * 6, out_specs=(*[HB] *...  2.47 us
    pallas_call x1, Pallas kernels, unpack(): pl.pallas_call(late_kernel, in_specs=[SM, VM, VM] + [HB] * 4 + [VM] * 3,...  2.11 us
  transfers between devices with their start and end apart: 18, of which 10 were waited for; matrix products, arithmetic and copies ran while one was open for 1% of the time, Pallas kernels for 7%

profile of v4, /device:TPU:1, one launch (start us, length us, event | category | flops | bytes accessed | tf_op | source)
XLA Modules:
  0.0 86.9 jit_solution(2043044786910284948)
XLA Ops:
  0.7 3.4 %shard_map.415 = (f32[3,4,192,256]{3,2,1,0:T(8,128)S(1)}, f32[3,776,256]{2,1,0:T(8,128)S(1)}) custom-call(s32[3]{0:T(128)S(1)} %pad_add_fusion.at_ref, f32[4,4,64,512]{3,2,1,0:T(8,128)} %bitcast.93, f32[4,4,64,128]{3,2,1,0:T(8,128)} %bitcast.95, f32[4,4,64,128]{3,2,1,0:T(8,128)} %bitcast.97, f32[1024,128]{1,0:T(8,128)} %bitcast.99, f32[1,512,1024]{2,1,0:T(8,128)} %down.3, ...), custom_call_target="tpu_custom_call" | custom-call | tf_op jit(solution)/shard_map/pallas_call | solution.py:143
  4.4 2.5 %collective-permute-start = (f16[768,256]{1,0:T(8,128)(2,1)S(1)}, f16[768,256]{1,0:T(8,128)(2,1)S(1)}, u32[]{:S(2)}, u32[]{:S(2)}) collective-permute-start(f16[768,256]{1,0:T(8,128)(2,1)S(1)} %bitcast.102), channel_id=1, source_target_pairs={{0,8},{1,33},{2,10},{3,35},{4,12},{5,37},{6,14},{7,39},{8,16},{9,4... | collective-permute-start | bytes 1179656 | tf_op jit(solution)/shard_map/ppermute | solution.py:50
  7.1 2.2 %collective-permute-start.1 = (f16[776,256]{1,0:T(8,128)(2,1)S(1)}, f16[776,256]{1,0:T(8,128)(2,1)S(1)}, u32[]{:S(2)}, u32[]{:S(2)}) collective-permute-start(f16[776,256]{1,0:T(8,128)(2,1)S(1)} %get-tuple-element.97), channel_id=1, source_target_pairs={{0,24},{1,97},{2,26},{3,99},{4,28},{5,101},{6,30},{7,103},{8,0},{9... | collective-permute-start | bytes 1191944 | tf_op jit(solution)/shard_map/ppermute | solution.py:50
  9.3 1.5 %collective-permute-start.2 = (f16[768,256]{1,0:T(8,128)(2,1)S(1)}, f16[768,256]{1,0:T(8,128)(2,1)S(1)}, u32[]{:S(2)}, u32[]{:S(2)}) collective-permute-start(f16[768,256]{1,0:T(8,128)(2,1)S(1)} %bitcast.101), channel_id=1, source_target_pairs={{0,24},{1,97},{2,26},{3,99},{4,28},{5,101},{6,30},{7,103},{8,0},{9... | collective-permute-start | bytes 1179656 | tf_op jit(solution)/shard_map/ppermute | solution.py:50
  10.8 3.7 %collective-permute-done = f16[768,256]{1,0:T(8,128)(2,1)S(1)} collective-permute-done((f16[768,256]{1,0:T(8,128)(2,1)S(1)}, f16[768,256]{1,0:T(8,128)(2,1)S(1)}, u32[]{:S(2)}, u32[]{:S(2)}) %collective-permute-start) | collective-permute-done | bytes 393248 | tf_op jit(solution)/shard_map/ppermute | solution.py:50
  14.9 2.9 %collective-permute-start.5 = (f16[776,256]{1,0:T(8,128)(2,1)S(1)}, f16[776,256]{1,0:T(8,128)(2,1)S(1)}, u32[]{:S(2)}, u32[]{:S(2)}) collective-permute-start(f16[776,256]{1,0:T(8,128)(2,1)S(1)} %fusion.3), channel_id=1, source_target_pairs={{0,24},{1,97},{2,26},{3,99},{4,28},{5,101},{6,30},{7,103},{8,0},{9... | collective-permute-start | bytes 1191944 | tf_op jit(solution)/shard_map/ppermute | solution.py:50
  17.7 2.7 %shard_map.416 = (f32[1,4,192,256]{3,2,1,0:T(8,128)S(1)}, f32[1,776,256]{2,1,0:T(8,128)S(1)}) custom-call(s32[3]{0:T(128)S(1)} %pad_add_fusion.at_ref, f32[4,4,64,512]{3,2,1,0:T(8,128)} %bitcast.94, f32[4,4,64,128]{3,2,1,0:T(8,128)} %bitcast.96, f32[4,4,64,128]{3,2,1,0:T(8,128)} %bitcast.98, f32[1024,128]{1,0:T(8,128)} %bitcast.100, f32[1,512,1024]{2,1,0:T(8,128)} %down.3, ...), custom_call_target="tpu_custom_call" | custom-call | tf_op jit(solution)/shard_map/pallas_call | solution.py:143
  20.5 2.7 %collective-permute-done.3 = f16[768,256]{1,0:T(8,128)(2,1)S(1)} collective-permute-done((f16[768,256]{1,0:T(8,128)(2,1)S(1)}, f16[768,256]{1,0:T(8,128)(2,1)S(1)}, u32[]{:S(2)}, u32[]{:S(2)}) %collective-permute-start.3) | collective-permute-done | bytes 393248 | tf_op jit(solution)/shard_map/ppermute | solution.py:50
  24.8 2.7 %collective-permute-start.6 = (f16[776,128]{1,0:T(8,128)(2,1)S(1)}, f16[776,128]{1,0:T(8,128)(2,1)S(1)}, u32[]{:S(2)}, u32[]{:S(2)}) collective-permute-start(f16[776,128]{1,0:T(8,128)(2,1)S(1)} %get-tuple-element.101), channel_id=1, source_target_pairs={{0,64},{1,17},{2,66},{3,19},{4,68},{5,21},{6,70},{7,23},{8,72},{9,... | collective-permute-start | bytes 595976 | tf_op jit(solution)/shard_map/ppermute | solution.py:50
  29.0 2.0 %collective-permute-done.6 = f16[776,128]{1,0:T(8,128)(2,1)S(1)} collective-permute-done((f16[776,128]{1,0:T(8,128)(2,1)S(1)}, f16[776,128]{1,0:T(8,128)(2,1)S(1)}, u32[]{:S(2)}, u32[]{:S(2)}) %collective-permute-start.6) | collective-permute-done | bytes 198688 | tf_op jit(solution)/shard_map/ppermute | solution.py:50
  31.0 2.5 %collective-permute-done.8 = f16[776,128]{1,0:T(8,128)(2,1)S(1)} collective-permute-done((f16[776,128]{1,0:T(8,128)(2,1)S(1)}, f16[776,128]{1,0:T(8,128)(2,1)S(1)}, u32[]{:S(2)}, u32[]{:S(2)}) %collective-permute-start.8) | collective-permute-done | bytes 198688 | tf_op jit(solution)/shard_map/ppermute | solution.py:50
  34.5 12.6 %all_to_all.5.parts = f32[8,16,128]{2,1,0:T(8,128)S(1)} all-to-all(f32[8,16,128]{2,1,0:T(8,128)S(1)} %norms.1), channel_id=1, replica_groups=mesh['replica'=16,'model'=8] {'model'}, dimensions={0} | all-to-all | bytes 131072 | tf_op jit(solution)/shard_map/all_to_all | solution.py:435
  47.5 2.8 %collective-permute-start.10 = (bf16[776,128]{1,0:T(8,128)(2,1)S(1)}, bf16[776,128]{1,0:T(8,128)(2,1)S(1)}, u32[]{:S(2)}, u32[]{:S(2)}) collective-permute-start(bf16[776,128]{1,0:T(8,128)(2,1)S(1)} %halves.1), channel_id=1, source_target_pairs={{0,96},{1,25},{2,98},{3,27},{4,100},{5,29},{6,102},{7,31},{8,104},... | collective-permute-start | bytes 595976 | tf_op jit(solution)/shard_map/ppermute | solution.py:50
  50.3 4.8 %collective-permute-done.10 = bf16[776,128]{1,0:T(8,128)(2,1)S(1)} collective-permute-done((bf16[776,128]{1,0:T(8,128)(2,1)S(1)}, bf16[776,128]{1,0:T(8,128)(2,1)S(1)}, u32[]{:S(2)}, u32[]{:S(2)}) %collective-permute-start.10) | collective-permute-done | bytes 198688 | tf_op jit(solution)/shard_map/ppermute | solution.py:50
  55.1 1.6 %collective-permute-done.9 = bf16[776,128]{1,0:T(8,128)(2,1)S(1)} collective-permute-done((bf16[776,128]{1,0:T(8,128)(2,1)S(1)}, bf16[776,128]{1,0:T(8,128)(2,1)S(1)}, u32[]{:S(2)}, u32[]{:S(2)}) %collective-permute-start.9) | collective-permute-done | bytes 198688 | tf_op jit(solution)/shard_map/ppermute | solution.py:50
  56.9 2.6 %collective-permute-start.17 = (bf16[3,776,128]{2,1,0:T(8,128)(2,1)S(1)}, bf16[3,776,128]{2,1,0:T(8,128)(2,1)S(1)}, u32[]{:S(2)}, u32[]{:S(2)}) collective-permute-start(bf16[3,776,128]{2,1,0:T(8,128)(2,1)S(1)} %pad_maximum_fusion.refs_0_), channel_id=1, source_target_pairs={{0,24},{1,97},{2,26},{3,99},{4,28},{5,101},{6,30},{7,103},{8,0},{9... | collective-permute-start | bytes 1787912 | tf_op jit(solution)/shard_map/ppermute | solution.py:50
  59.5 9.8 %collective-permute-done.11.refs_2_ = bf16[3,776,128]{2,1,0:T(8,128)(2,1)S(1)} collective-permute-done((bf16[3,776,128]{2,1,0:T(8,128)(2,1)S(1)}, bf16[3,776,128]{2,1,0:T(8,128)(2,1)S(1)}, u32[]{:S(2)}, u32[]{:S(2)}) %collective-permute-start.11) | collective-permute-done | bytes 596000 | tf_op jit(solution)/shard_map/ppermute | solution.py:50
  69.2 2.7 %collective-permute-start.14 = (bf16[1,776,128]{2,1,0:T(8,128)(2,1)S(1)}, bf16[1,776,128]{2,1,0:T(8,128)(2,1)S(1)}, u32[]{:S(2)}, u32[]{:S(2)}) collective-permute-start(bf16[1,776,128]{2,1,0:T(8,128)(2,1)S(1)} %bitcast.80), channel_id=1, source_target_pairs={{0,24},{1,97},{2,26},{3,99},{4,28},{5,101},{6,30},{7,103},{8,0},{9... | collective-permute-start | bytes 595976 | tf_op jit(solution)/shard_map/ppermute | solution.py:50
  71.9 2.6 %collective-permute-done.14.refs_5_ = bf16[1,776,128]{2,1,0:T(8,128)(2,1)S(1)} collective-permute-done((bf16[1,776,128]{2,1,0:T(8,128)(2,1)S(1)}, bf16[1,776,128]{2,1,0:T(8,128)(2,1)S(1)}, u32[]{:S(2)}, u32[]{:S(2)}) %collective-permute-start.14) | collective-permute-done | bytes 198688 | tf_op jit(solution)/shard_map/ppermute | solution.py:50
  74.6 3.4 %collective-permute-start.15 = (bf16[1,776,128]{2,1,0:T(8,128)(2,1)S(1)}, bf16[1,776,128]{2,1,0:T(8,128)(2,1)S(1)}, u32[]{:S(2)}, u32[]{:S(2)}) collective-permute-start(bf16[1,776,128]{2,1,0:T(8,128)(2,1)S(1)} %collective-permute-done.14.refs_5_), channel_id=1, source_target_pairs={{0,24},{1,97},{2,26},{3,99},{4,28},{5,101},{6,30},{7,103},{8,0},{9... | collective-permute-start | bytes 595976 | tf_op jit(solution)/shard_map/ppermute | solution.py:50
  78.0 1.2 %update.1 = (f32[64,512]{1,0:T(8,128)}, f32[64,128]{1,0:T(8,128)}, f32[64,128]{1,0:T(8,128)}, f32[64,128]{1,0:T(8,128)}, f32[64,512]{1,0:T(8,128)}, /*index=5*/f...) custom-call(f32[8,16,128]{2,1,0:T(8,128)S(1)} %all_to_all.5.parts, ...), custom_call_target="tpu_custom_call" | custom-call | tf_op jit(solution)/shard_map/update/pallas_call | solution.py:286
  79.1 2.5 %collective-permute-done.16.refs_3_ = bf16[1,776,128]{2,1,0:T(8,128)(2,1)S(1)} collective-permute-done((bf16[1,776,128]{2,1,0:T(8,128)(2,1)S(1)}, bf16[1,776,128]{2,1,0:T(8,128)(2,1)S(1)}, u32[]{:S(2)}, u32[]{:S(2)}) %collective-permute-start.16) | collective-permute-done | bytes 198688 | tf_op jit(solution)/shard_map/ppermute | solution.py:50
  81.7 2.5 %unpack_early.1 = (bf16[1024,512]{1,0:T(8,128)(2,1)}, bf16[1024,128]{1,0:T(8,128)(2,1)}, bf16[1024,128]{1,0:T(8,128)(2,1)}, bf16[1024,128]{1,0:T(8,128)(2,1)}, b...) custom-call(s32[3]{0:T(128)S(1)} %pad_add_fusion.at_ref, ...), custom_call_target="tpu_custom_call" | custom-call | tf_op jit(solution)/shard_map/unpack_early/pallas_call | solution.py:372
  84.2 2.1 %unpack_late.1 = (bf16[1024,512]{1,0:T(8,128)(2,1)}, bf16[1024,128]{1,0:T(8,128)(2,1)}, bf16[1024,128]{1,0:T(8,128)(2,1)}, bf16[1024,128]{1,0:T(8,128)(2,1)}, bf...) custom-call(s32[3]{0:T(128)S(1)} %pad_add_fusion.at_ref, ...), custom_call_target="tpu_custom_call", output_to_operand_aliasing={{0}: (3, {}), {1}: (4, {}), {2}: (5, {}), {3}: (6, {}), {4}... | custom-call | tf_op jit(solution)/shard_map/unpack_late/pallas_call | solution.py:385
  (67 shorter events, 6.1 us)
Async XLA Ops:
  4.4 10.0 %collective-permute-start = (f16[768,256]{1,0:T(8,128)(2,1)S(1)}, f16[768,256]{1,0:T(8,128)(2,1)S(1)}, u32[]{:S(2)}, u32[]{:S(2)}) collective-permute-start(f16[768,256]{1,0:T(8,128)(2,1)S(1)} %bitcast.102), channel_id=1, source_target_pairs={{0,8},{1,33},{2,10},{3,35},{4,12},{5,37},{6,14},{7,39},{8,16},{9,4... | collective-permute-start | bytes 1179656 | tf_op jit(solution)/shard_map/ppermute | solution.py:50
  7.1 7.6 %collective-permute-start.1 = (f16[776,256]{1,0:T(8,128)(2,1)S(1)}, f16[776,256]{1,0:T(8,128)(2,1)S(1)}, u32[]{:S(2)}, u32[]{:S(2)}) collective-permute-start(f16[776,256]{1,0:T(8,128)(2,1)S(1)} %get-tuple-element.97), channel_id=1, source_target_pairs={{0,24},{1,97},{2,26},{3,99},{4,28},{5,101},{6,30},{7,103},{8,0},{9... | collective-permute-start | bytes 1191944 | tf_op jit(solution)/shard_map/ppermute | solution.py:50
  9.3 11.2 %collective-permute-start.2 = (f16[768,256]{1,0:T(8,128)(2,1)S(1)}, f16[768,256]{1,0:T(8,128)(2,1)S(1)}, u32[]{:S(2)}, u32[]{:S(2)}) collective-permute-start(f16[768,256]{1,0:T(8,128)(2,1)S(1)} %bitcast.101), channel_id=1, source_target_pairs={{0,24},{1,97},{2,26},{3,99},{4,28},{5,101},{6,30},{7,103},{8,0},{9... | collective-permute-start | bytes 1179656 | tf_op jit(solution)/shard_map/ppermute | solution.py:50
  10.7 12.6 %collective-permute-start.4 = (f16[776,256]{1,0:T(8,128)(2,1)S(1)}, f16[776,256]{1,0:T(8,128)(2,1)S(1)}, u32[]{:S(2)}, u32[]{:S(2)}) collective-permute-start(f16[776,256]{1,0:T(8,128)(2,1)S(1)} %get-tuple-element.96), channel_id=1, source_target_pairs={{0,8},{1,33},{2,10},{3,35},{4,12},{5,37},{6,14},{7,39},{8,16},{9,4... | collective-permute-start | bytes 1191944 | tf_op jit(solution)/shard_map/ppermute | solution.py:50
  14.6 8.6 %collective-permute-start.3 = (f16[768,256]{1,0:T(8,128)(2,1)S(1)}, f16[768,256]{1,0:T(8,128)(2,1)S(1)}, u32[]{:S(2)}, u32[]{:S(2)}) collective-permute-start(f16[768,256]{1,0:T(8,128)(2,1)S(1)} %fusion.7), channel_id=1, source_target_pairs={{0,8},{1,33},{2,10},{3,35},{4,12},{5,37},{6,14},{7,39},{8,16},{9,4... | collective-permute-start | bytes 1179656 | tf_op jit(solution)/shard_map/ppermute | solution.py:50
  14.9 8.5 %collective-permute-start.5 = (f16[776,256]{1,0:T(8,128)(2,1)S(1)}, f16[776,256]{1,0:T(8,128)(2,1)S(1)}, u32[]{:S(2)}, u32[]{:S(2)}) collective-permute-start(f16[776,256]{1,0:T(8,128)(2,1)S(1)} %fusion.3), channel_id=1, source_target_pairs={{0,24},{1,97},{2,26},{3,99},{4,28},{5,101},{6,30},{7,103},{8,0},{9... | collective-permute-start | bytes 1191944 | tf_op jit(solution)/shard_map/ppermute | solution.py:50
  24.6 22.5 %copy-start.2 = (f32[64,512]{1,0:T(8,128)S(1)}, f32[64,512]{1,0:T(8,128)}, u32[]{:S(2)}) copy-start(f32[64,512]{1,0:T(8,128)} %refs_8_.3) | copy-start | bytes 393220
  24.6 22.5 %copy-start.3 = (f32[512,64]{0,1:T(8,128)S(1)}, f32[512,64]{0,1:T(8,128)}, u32[]{:S(2)}) copy-start(f32[512,64]{0,1:T(8,128)} %param.41) | copy-start | bytes 393220
  24.6 22.5 %copy-start.8 = (f32[64,128]{1,0:T(8,128)S(1)}, f32[64,128]{1,0:T(8,128)}, u32[]{:S(2)}) copy-start(f32[64,128]{1,0:T(8,128)} %refs_9_.3) | copy-start | bytes 98308
  24.6 22.5 %copy-start.9 = (f32[64,128]{1,0:T(8,128)S(1)}, f32[64,128]{1,0:T(8,128)}, u32[]{:S(2)}) copy-start(f32[64,128]{1,0:T(8,128)} %refs_10_.3) | copy-start | bytes 98308
  24.6 22.5 %copy-start.10 = (f32[64,128]{1,0:T(8,128)S(1)}, f32[64,128]{1,0:T(8,128)}, u32[]{:S(2)}) copy-start(f32[64,128]{1,0:T(8,128)} %refs_11_.3) | copy-start | bytes 98308
  24.6 22.5 %copy-start.11 = (f32[128,64]{0,1:T(8,128)S(1)}, f32[128,64]{0,1:T(8,128)}, u32[]{:S(2)}) copy-start(f32[128,64]{0,1:T(8,128)} %param.45) | copy-start | bytes 98308
  24.8 6.1 %collective-permute-start.6 = (f16[776,128]{1,0:T(8,128)(2,1)S(1)}, f16[776,128]{1,0:T(8,128)(2,1)S(1)}, u32[]{:S(2)}, u32[]{:S(2)}) collective-permute-start(f16[776,128]{1,0:T(8,128)(2,1)S(1)} %get-tuple-element.101), channel_id=1, source_target_pairs={{0,64},{1,17},{2,66},{3,19},{4,68},{5,21},{6,70},{7,23},{8,72},{9,... | collective-permute-start | bytes 595976 | tf_op jit(solution)/shard_map/ppermute | solution.py:50
  27.5 5.9 %collective-permute-start.8 = (f16[776,128]{1,0:T(8,128)(2,1)S(1)}, f16[776,128]{1,0:T(8,128)(2,1)S(1)}, u32[]{:S(2)}, u32[]{:S(2)}) collective-permute-start(f16[776,128]{1,0:T(8,128)(2,1)S(1)} %get-tuple-element.102), channel_id=1, source_target_pairs={{0,96},{1,25},{2,98},{3,27},{4,100},{5,29},{6,102},{7,31},{8,104},... | collective-permute-start | bytes 595976 | tf_op jit(solution)/shard_map/ppermute | solution.py:50
  28.3 5.8 %collective-permute-start.7 = (f16[776,128]{1,0:T(8,128)(2,1)S(1)}, f16[776,128]{1,0:T(8,128)(2,1)S(1)}, u32[]{:S(2)}, u32[]{:S(2)}) collective-permute-start(f16[776,128]{1,0:T(8,128)(2,1)S(1)} %get-tuple-element.103), channel_id=1, source_target_pairs={{0,32},{1,9},{2,34},{3,11},{4,36},{5,13},{6,38},{7,15},{8,40},{9,1... | collective-permute-start | bytes 595976 | tf_op jit(solution)/shard_map/ppermute | solution.py:50
  47.5 7.6 %collective-permute-start.10 = (bf16[776,128]{1,0:T(8,128)(2,1)S(1)}, bf16[776,128]{1,0:T(8,128)(2,1)S(1)}, u32[]{:S(2)}, u32[]{:S(2)}) collective-permute-start(bf16[776,128]{1,0:T(8,128)(2,1)S(1)} %halves.1), channel_id=1, source_target_pairs={{0,96},{1,25},{2,98},{3,27},{4,100},{5,29},{6,102},{7,31},{8,104},... | collective-permute-start | bytes 595976 | tf_op jit(solution)/shard_map/ppermute | solution.py:50
  50.3 6.3 %collective-permute-start.9 = (bf16[776,128]{1,0:T(8,128)(2,1)S(1)}, bf16[776,128]{1,0:T(8,128)(2,1)S(1)}, u32[]{:S(2)}, u32[]{:S(2)}) collective-permute-start(bf16[776,128]{1,0:T(8,128)(2,1)S(1)} %halves.1), channel_id=1, source_target_pairs={{0,64},{1,17},{2,66},{3,19},{4,68},{5,21},{6,70},{7,23},{8,72},{9,... | collective-permute-start | bytes 595976 | tf_op jit(solution)/shard_map/ppermute | solution.py:50
  56.7 12.5 %collective-permute-start.11 = (bf16[3,776,128]{2,1,0:T(8,128)(2,1)S(1)}, bf16[3,776,128]{2,1,0:T(8,128)(2,1)S(1)}, u32[]{:S(2)}, u32[]{:S(2)}) collective-permute-start(bf16[3,776,128]{2,1,0:T(8,128)(2,1)S(1)} %pad_maximum_fusion.refs_0_), channel_id=1, source_target_pairs={{0,8},{1,33},{2,10},{3,35},{4,12},{5,37},{6,14},{7,39},{8,16},{9,4... | collective-permute-start | bytes 1787912 | tf_op jit(solution)/shard_map/ppermute | solution.py:50
  56.8 12.4 %collective-permute-start.13 = (bf16[776,128]{1,0:T(8,128)(2,1)S(1)}, bf16[776,128]{1,0:T(8,128)(2,1)S(1)}, u32[]{:S(2)}, u32[]{:S(2)}) collective-permute-start(bf16[776,128]{1,0:T(8,128)(2,1)S(1)} %halves.1), channel_id=1, source_target_pairs={{0,32},{1,9},{2,34},{3,11},{4,36},{5,13},{6,38},{7,15},{8,40},{9,1... | collective-permute-start | bytes 595976 | tf_op jit(solution)/shard_map/ppermute | solution.py:50
  56.9 24.8 %collective-permute-start.17 = (bf16[3,776,128]{2,1,0:T(8,128)(2,1)S(1)}, bf16[3,776,128]{2,1,0:T(8,128)(2,1)S(1)}, u32[]{:S(2)}, u32[]{:S(2)}) collective-permute-start(bf16[3,776,128]{2,1,0:T(8,128)(2,1)S(1)} %pad_maximum_fusion.refs_0_), channel_id=1, source_target_pairs={{0,24},{1,97},{2,26},{3,99},{4,28},{5,101},{6,30},{7,103},{8,0},{9... | collective-permute-start | bytes 1787912 | tf_op jit(solution)/shard_map/ppermute | solution.py:50
  69.2 14.9 %collective-permute-start.12 = (bf16[3,776,128]{2,1,0:T(8,128)(2,1)S(1)}, bf16[3,776,128]{2,1,0:T(8,128)(2,1)S(1)}, u32[]{:S(2)}, u32[]{:S(2)}) collective-permute-start(bf16[3,776,128]{2,1,0:T(8,128)(2,1)S(1)} %collective-permute-done.11.refs_2_), channel_id=1, source_target_pairs={{0,8},{1,33},{2,10},{3,35},{4,12},{5,37},{6,14},{7,39},{8,16},{9,4... | collective-permute-start | bytes 1787912 | tf_op jit(solution)/shard_map/ppermute | solution.py:50
  69.2 5.3 %collective-permute-start.14 = (bf16[1,776,128]{2,1,0:T(8,128)(2,1)S(1)}, bf16[1,776,128]{2,1,0:T(8,128)(2,1)S(1)}, u32[]{:S(2)}, u32[]{:S(2)}) collective-permute-start(bf16[1,776,128]{2,1,0:T(8,128)(2,1)S(1)} %bitcast.80), channel_id=1, source_target_pairs={{0,24},{1,97},{2,26},{3,99},{4,28},{5,101},{6,30},{7,103},{8,0},{9... | collective-permute-start | bytes 595976 | tf_op jit(solution)/shard_map/ppermute | solution.py:50
  71.9 9.8 %collective-permute-start.16 = (bf16[1,776,128]{2,1,0:T(8,128)(2,1)S(1)}, bf16[1,776,128]{2,1,0:T(8,128)(2,1)S(1)}, u32[]{:S(2)}, u32[]{:S(2)}) collective-permute-start(bf16[1,776,128]{2,1,0:T(8,128)(2,1)S(1)} %bitcast.81), channel_id=1, source_target_pairs={{0,8},{1,33},{2,10},{3,35},{4,12},{5,37},{6,14},{7,39},{8,16},{9,4... | collective-permute-start | bytes 595976 | tf_op jit(solution)/shard_map/ppermute | solution.py:50
  74.6 9.6 %collective-permute-start.15 = (bf16[1,776,128]{2,1,0:T(8,128)(2,1)S(1)}, bf16[1,776,128]{2,1,0:T(8,128)(2,1)S(1)}, u32[]{:S(2)}, u32[]{:S(2)}) collective-permute-start(bf16[1,776,128]{2,1,0:T(8,128)(2,1)S(1)} %collective-permute-done.14.refs_5_), channel_id=1, source_target_pairs={{0,24},{1,97},{2,26},{3,99},{4,28},{5,101},{6,30},{7,103},{8,0},{9... | collective-permute-start | bytes 595976 | tf_op jit(solution)/shard_map/ppermute | solution.py:50
  (10 other events, 148.5 us)
